TPU v7x, 32 devices: a 4x2x2 block of a 4x4x8 slice. The times are simulated.
32 devices in a mesh: dp: 4 (over y, z), tp: 8 (over x, core).
Axes of the slice: x: 4, y: 2, z: 2, core: 2. Of those that a mesh axis runs over, the one named last changes fastest.
The devices are a block of a 4x4x8 slice.
Arguments:
- hidden: bfloat16 [8192, 2048], P(('dp', 'tp')), parts along dimension 0
- w_two: bfloat16 [2048, 2048], replicated
- ln_scale: float32 [2, 2048], replicated
- ln_shift: float32 [2, 2048], replicated
- embed: bfloat16 [32768, 2048], P('tp')
- targets: int32 [2, 8192], P(None, ('dp', 'tp')), parts along dimension 1
- loss_mask: int32 [2, 8192], P(None, ('dp', 'tp')), parts along dimension 1
Outputs:
- output 1: float32 [2, 8192], P(None, ('dp', 'tp')), parts along dimension 1
- output 2: float32 [4], P('dp'), parts along dimension 0
- output 3: bfloat16 [8192, 2048], P(('dp', 'tp')), parts along dimension 0
- output 4: float32 [131072, 2048], P(('dp', 'tp')), parts along dimension 0
- output 5: float32 [8192, 2048], P('dp'), parts along dimension 0
- output 6: float32 [8, 2048], P('dp'), parts along dimension 0
- output 7: float32 [8, 2048], P('dp'), parts along dimension 0
There are 4 independent parts. A program takes and returns all parts, laid end to end along the dimension named above; an argument that names none is the same for every part.
All inputs are finite; a program needn't handle non-finite values.
Results may differ from a plain program's by a relative error of at most 0.00168.
Values are sent between devices in bfloat16 or wider.
A program may use at most 768 MiB of HBM per device.

v0:
```python
import jax
import jax.numpy as jnp
from jax import lax
from jax.sharding import PartitionSpec as P

LN_EPS = 1e-5


def layer_norm(values, gain, bias):
    mean_val = jnp.mean(values, axis=-1, keepdims=True)
    centered = values - mean_val
    variance = jnp.mean(centered * centered, axis=-1, keepdims=True)
    return centered * lax.rsqrt(variance + LN_EPS) * gain + bias


def solution(mesh):
    tok_spec = P(('dp', 'tp'), None)
    row_spec = P(None, ('dp', 'tp'))

    def device_step(hidden, w_two, ln_scale, ln_shift, embed, targets, loss_mask):
        tok_rows = hidden.shape[0]
        shard_rows = embed.shape[0]
        shard_idx = lax.axis_index('tp')
        proj_out = jnp.dot(hidden, w_two, preferred_element_type=jnp.float32).astype(jnp.bfloat16)
        norm_input = jnp.stack([hidden.astype(jnp.float32), proj_out.astype(jnp.float32)])
        normed, ln_back = jax.vjp(jax.vmap(layer_norm), norm_input, ln_scale, ln_shift)
        x_loc = normed.astype(jnp.bfloat16)
        x_all = lax.all_gather(x_loc, 'tp', axis=1, tiled=True)
        int_all = lax.all_gather(jnp.stack([targets, loss_mask]), 'tp', axis=2, tiled=True)
        tgt_all = int_all[0]
        mask_all = int_all[1].astype(jnp.float32)
        logits = jnp.einsum('hsd,vd->hsv', x_all, embed, preferred_element_type=jnp.float32)
        local_max = jnp.max(logits, axis=-1)
        exp_loc = jnp.exp(logits - local_max[..., None])
        col_ids = lax.broadcasted_iota(jnp.int32, (1, 1, shard_rows), 2) + shard_idx * shard_rows
        is_target = col_ids == tgt_all[..., None]
        tgt_loc = jnp.sum(jnp.where(is_target, logits, 0.0), axis=-1)
        glob_max = lax.pmax(local_max, 'tp')
        part_stats = jnp.stack([jnp.sum(exp_loc, axis=-1) * jnp.exp(local_max - glob_max), tgt_loc])
        glob_stats = lax.psum(part_stats, 'tp')
        log_norm = glob_max + jnp.log(glob_stats[0])
        token_count = jnp.sum(mask_all, axis=1)
        weight = mask_all / token_count[:, None]
        loss_all = (log_norm - glob_stats[1]) * mask_all
        total_loss = jnp.sum(loss_all / token_count[:, None]).reshape(1)
        token_loss = lax.dynamic_slice_in_dim(loss_all, shard_idx * tok_rows, tok_rows, axis=1)
        softmax_val = exp_loc * jnp.exp(local_max - log_norm)[..., None]
        d_logits = (jnp.where(is_target, softmax_val - 1.0, softmax_val) * weight[..., None]).astype(jnp.bfloat16)
        d_embed = jnp.einsum('hsv,hsd->vd', d_logits, x_all, preferred_element_type=jnp.float32)
        dx_part = jnp.einsum('hsv,vd->hsd', d_logits, embed, preferred_element_type=jnp.float32)
        dx_loc = lax.psum_scatter(dx_part, 'tp', scatter_dimension=1, tiled=True)
        d_norm_in, d_scale_part, d_shift_part = ln_back(dx_loc)
        d_proj = d_norm_in[1].astype(jnp.bfloat16)
        d_hidden = (d_norm_in[0] + jnp.einsum('td,ed->te', d_proj, w_two, preferred_element_type=jnp.float32)).astype(jnp.bfloat16)
        d_w_part = jnp.einsum('te,td->ed', hidden, d_proj, preferred_element_type=jnp.float32)
        d_w_two, d_scale, d_shift = lax.psum((d_w_part, d_scale_part, d_shift_part), 'tp')
        return token_loss, total_loss, d_hidden, d_embed, d_w_two, d_scale, d_shift

    return jax.shard_map(device_step, mesh=mesh,
                         in_specs=(tok_spec, P(), P(), P(), P('tp', None), row_spec, row_spec),
                         out_specs=(row_spec, P('dp'), tok_spec, tok_spec, P('dp', None), P('dp', None), P('dp', None)),
                         check_vma=False)
```

profile of v0, /device:TPU:81, one launch (start us, length us, event | category | flops | bytes accessed | tf_op | source)
XLA Modules:
  0.0 725.0 jit_solution(857607465027438303)
XLA Ops:
  7.3 6.1 fusion.20
  13.8 0.7 fusion.17
  15.7 2.3 fusion.15
  18.1 15.0 %all_gather.7 = s32[2,2,2048]{2,1,0:T(2,128)S(1)} all-gather(s32[2,2,256]{2,1,0:T(2,128)S(1)} %pad_add_fusion), channel_id=1, replica_groups=mesh['dp'=4,'tp'=8] {'tp'}, dimensions={2}, use_global_device_ids=true | all-gather | bytes 36864 | tf_op jit(solution)/shard_map/all_gather | solution.py:29
  33.7 0.6 fusion.29
  34.9 69.8 %all-gather.2.cloned.1.call-done = bf16[2,2048,2048]{2,1,0:T(8,128)(2,1)} async-done(((bf16[2,256,2048]{2,1,0:T(8,128)(2,1)}), bf16[2,2048,2048]{2,1,0:T(8,128)(2,1)}) %all-gather.2.cloned.1.call-update) | async-done | bytes 16777232 | tf_op jit(solution)/shard_map/all_gather | solution.py:28
  104.8 79.5 %fusion.35 = (f32[2,2048]{1,0:T(2,128)S(1)}, f32[2,2048,4096]{2,1,0:T(8,128)}) fusion(bf16[2,2048,2048]{2,1,0:T(8,128)(2,1)} %all-gather.2.cloned.1.call-done, bf16[4096,2048]{1,0:T(8,128)(2,1)} %param.11), kind=kOutput, calls=%fused_computation.60 | convolution fusion | flops 68736253952 | bytes 100679680 | tf_op jit(solution)/shard_map/hsd,vd->hsv/dot_general | solution.py:32
  184.3 21.2 %pmax.7 = f32[2,2048]{1,0:T(2,128)S(1)} all-reduce(f32[2,2048]{1,0:T(2,128)S(1)} %get-tuple-element.26), channel_id=1, replica_groups=mesh['dp'=4,'tp'=8] {'tp'}, use_global_device_ids=true, to_apply=%region_3.4 | all-reduce | flops 4096 | bytes 32768 | tf_op jit(solution)/shard_map/pmax | solution.py:38
  205.5 21.5 %fusion.3 = (f32[2,2048]{1,0:T(2,128)S(1)}, f32[2,2048]{1,0:T(2,128)S(1)}) fusion(f32[2,2048,4096]{2,1,0:T(8,128)} %get-tuple-element.27, f32[2,2048]{1,0:T(2,128)S(1)} %get-tuple-element.26, s32[2,2048]{1,0:T(2,128)S(1)} %copy-done.15, s32[4096]{0:T(1024)S(1)} %copy-done.14), kind=kLoop, calls=%fused_computation.6 | loop fusion | flops 83877888 | bytes 67190784 | tf_op jit(solution)/shard_map/reduce_sum | solution.py:39
  227.1 23.9 %psum.28 = f32[2,2,2048]{2,1,0:T(2,128)S(1)} all-reduce(f32[2,2,2048]{2,1,0:T(2,128)S(1)} %pad_maximum_fusion.1), channel_id=1, replica_groups=mesh['dp'=4,'tp'=8] {'tp'}, use_global_device_ids=true, to_apply=%region_6.7 | all-reduce | flops 8192 | bytes 65536 | tf_op jit(solution)/shard_map/psum | solution.py:40
  251.0 1.2 divide_reduce_fusion
  252.3 84.4 %fusion.4 = f32[2,2048,2048]{2,1,0:T(8,128)} fusion(bf16[4096,2048]{1,0:T(8,128)(2,1)} %param.11, f32[2,2048,4096]{2,1,0:T(8,128)} %get-tuple-element.27, f32[2,2048]{1,0:T(2,128)S(1)} %get-tuple-element.25, f32[2,2048]{1,0:T(2,128)S(1)} %get-tuple-element.24, s32[2,2048]{1,0:T(2,128)S(1)} %copy-done.15, s32[4096]{0:T(1024)S(1)} %copy-done.14, ...), kind=kOutput, calls=%fused_computation.8 | convolution fusion | flops 68836917248 | bytes 117522432 | tf_op jit(solution)/shard_map/hsv,vd->hsd/dot_general | solution.py:50
  337.1 1.5 constant_dynamic-slice_fusion
  338.6 167.1 %reduce-scatter.2.cloned.1.call-done = f32[2,256,2048]{2,1,0:T(8,128)} async-done(((f32[2,2048,2048]{2,1,0:T(8,128)}), f32[2,256,2048]{2,1,0:T(8,128)}) %reduce-scatter.2.cloned.1.call-update) | async-done | bytes 4194320 | tf_op jit(solution)/shard_map/reduce_scatter | solution.py:51
  505.7 3.9 fusion.33
  509.7 2.5 fusion.16
  512.1 1.5 broadcast_add_fusion
  513.7 1.9 copy-done.5
  515.6 8.5 %convolution_bitcast_fusion.1 = f32[2048,2048]{0,1:T(8,128)} fusion(bf16[256,2048]{1,0:T(8,128)(2,1)S(1)} %copy-done.1, f32[2,256,2048]{2,1,0:T(8,128)S(1)} %broadcast_add_fusion), kind=kOutput, calls=%fused_computation.12 | convolution fusion | flops 2147483648 | bytes 18874368 | tf_op jit(solution)/shard_map/te,td->ed/dot_general | solution.py:55
  524.2 105.4 %convolution_bitcast_fusion = f32[4096,2048]{1,0:T(8,128)} fusion(bf16[2,2048,2048]{2,1,0:T(8,128)(2,1)} %all-gather.2.cloned.1.call-done, f32[2,2048,4096]{2,1,0:T(8,128)} %get-tuple-element.27, f32[2,2048]{1,0:T(2,128)S(1)} %get-tuple-element.25, f32[2,2048]{1,0:T(2,128)S(1)} %get-tuple-element.24, s32[2,2048]{1,0:T(2,128)S(1)} %copy-done.15, ...), kind=kOutput, calls=%fused_computation.7 | convolution fusion | flops 68836917248 | bytes 117522432 | tf_op jit(solution)/shard_map/hsv,hsd->vd/dot_general | solution.py:49
  629.7 22.6 %all-reduce = (f32[2,2048]{1,0:T(2,128)}, f32[2,2048]{1,0:T(2,128)}) all-reduce(f32[2,2048]{1,0:T(2,128)S(1)} %copy-done.13, f32[2,2048]{1,0:T(2,128)S(1)} %copy-done.12), channel_id=1, replica_groups=mesh['dp'=4,'tp'=8] {'tp'}, use_global_device_ids=true, to_apply=%region_14.15 | all-reduce | flops 8192 | bytes 65536 | tf_op jit(solution)/shard_map/psum | solution.py:56
  652.3 7.9 %fusion.19 = bf16[256,2048]{1,0:T(8,128)(2,1)} fusion(bf16[2048,2048]{1,0:T(8,128)(2,1)} %param.8, f32[2,256,2048]{2,1,0:T(8,128)} %copy-done.5), kind=kOutput, calls=%fused_computation.28 | convolution fusion | flops 2149056512 | bytes 13631488 | tf_op jit(solution)/shard_map/td,ed->te/dot_general | solution.py:54
  660.2 40.6 %all-reduce.3.cloned.1.call-done = f32[2048,2048]{0,1:T(8,128)} async-done(((f32[2048,2048]{0,1:T(8,128)}), f32[2048,2048]{0,1:T(8,128)}) %all-reduce.3.cloned.1.call-update) | async-done | bytes 16777232 | tf_op jit(solution)/shard_map/psum | solution.py:56
  700.8 17.6 %copy.15 = f32[2048,2048]{1,0:T(8,128)} copy(f32[2048,2048]{0,1:T(8,128)} %all-reduce.3.cloned.1.call-done) | data formatting | bytes 33554432
  (63 shorter events, 3.5 us)
Async XLA Ops:
  7.2 6.2 copy-start
  7.2 97.6 %all-gather.2.cloned.1.call-start = ((), (), s32[]{:S(2)}) async-start(), calls=%async_computation.1 | async-start | bytes 18874368 | tf_op jit(solution)/shard_map/all_gather | solution.py:28
  13.4 1.7 copy-start.2
  13.4 2.3 copy-start.6
  13.4 2.3 copy-start.20
  13.8 1.3 copy-start.10
  13.8 4.3 copy-start.22
  13.8 4.3 copy-start.23
  18.0 487.7 %reduce-scatter.2.cloned.1.call-start = ((), (), s32[]{:S(2)}) async-start(), calls=%async_computation.2 | async-start | bytes 37748736 | tf_op jit(solution)/shard_map/reduce_scatter | solution.py:51
  104.8 100.8 %copy-start.14 = (s32[4096]{0:T(1024)S(1)}, s32[4096]{0:T(1024)}, u32[]{:S(2)}) copy-start(s32[4096]{0:T(1024)} %iota_add_fusion) | copy-start | bytes 49156
  104.8 100.8 %copy-start.15 = (s32[2,2048]{1,0:T(2,128)S(1)}, s32[2,2048]{1,0:T(2,128)}, u32[]{:S(2)}) copy-start(s32[2,2048]{1,0:T(2,128)} %slice_bitcast_fusion.2) | copy-start | bytes 49156
  205.5 45.5 %copy-start.9 = (s32[2,2,2048]{2,1,0:T(2,128)S(1)}, s32[2,2,2048]{2,1,0:T(2,128)}, u32[]{:S(2)}) copy-start(s32[2,2,2048]{2,1,0:T(2,128)} %copy-done.8) | copy-start | bytes 98308
  205.5 45.5 %copy-start.21 = (f32[2]{0:T(128)S(1)}, f32[2]{0:T(128)}, u32[]{:S(2)}) copy-start(f32[2]{0:T(128)} %fusion.29) | copy-start | bytes 28
  336.6 169.1 %copy-start.1 = (bf16[256,2048]{1,0:T(8,128)(2,1)S(1)}, bf16[256,2048]{1,0:T(8,128)(2,1)}, u32[]{:S(2)}) copy-start(bf16[256,2048]{1,0:T(8,128)(2,1)} %param.7) | copy-start | bytes 3145732
  336.6 169.1 %copy-start.3 = (bf16[1,256,2048]{2,1,0:T(8,128)(2,1)S(1)}, bf16[1,256,2048]{2,1,0:T(8,128)(2,1)}, u32[]{:S(2)}) copy-start(bf16[1,256,2048]{2,1,0:T(8,128)(2,1)} %copy-done.2) | copy-start | bytes 3145732
  336.6 169.1 %copy-start.7 = (f32[2,2048]{1,0:T(2,128)S(1)}, f32[2,2048]{1,0:T(2,128)}, u32[]{:S(2)}) copy-start(f32[2,2048]{1,0:T(2,128)} %param.9) | copy-start | bytes 49156
  336.6 169.1 %copy-start.11 = (f32[2,256]{1,0:T(2,128)S(1)}, f32[2,256]{1,0:T(2,128)}, u32[]{:S(2)}) copy-start(f32[2,256]{1,0:T(2,128)} %copy-done.10) | copy-start | bytes 6148
  336.7 172.9 %copy-start.19 = (f32[2,256]{1,0:T(2,128)S(1)}, f32[2,256]{1,0:T(2,128)}, u32[]{:S(2)}) copy-start(f32[2,256]{1,0:T(2,128)} %copy-done.18) | copy-start | bytes 6148
  336.7 172.9 %copy-start.17 = (f32[2,256]{1,0:T(2,128)S(1)}, f32[2,256]{1,0:T(2,128)}, u32[]{:S(2)}) copy-start(f32[2,256]{1,0:T(2,128)} %copy-done.16) | copy-start | bytes 6148
  336.7 364.1 %all-reduce.3.cloned.1.call-start = ((), (), s32[]{:S(2)}) async-start(), calls=%async_computation.3 | async-start | bytes 33554432 | tf_op jit(solution)/shard_map/psum | solution.py:56
  505.7 4.0 copy-start.4
  513.7 1.9 copy-start.5
  524.2 105.5 %copy-start.12 = (f32[2,2048]{1,0:T(2,128)S(1)}, f32[2,2048]{1,0:T(2,128)}, u32[]{:S(2)}) copy-start(f32[2,2048]{1,0:T(2,128)} %get-tuple-element.18) | copy-start | bytes 49156
  524.2 105.5 %copy-start.13 = (f32[2,2048]{1,0:T(2,128)S(1)}, f32[2,2048]{1,0:T(2,128)}, u32[]{:S(2)}) copy-start(f32[2,2048]{1,0:T(2,128)} %get-tuple-element.16) | copy-start | bytes 49156
  (3 other events, 2.4 us)
Sparse Core Ops, SparseCore 0:
  18.1 86.6 all-gather.1
  336.8 168.8 reduce-scatter.1
  524.3 176.4 all-reduce.2
where the time goes:
time: 725 us
  matrix products  292 us (40%)
  waiting for transfers between devices  278 us (38%)
  blocking collectives  82.7 us (11%)
  other arithmetic  35.3 us (5%)
  local copies, waits for them, and re-layouts  22.9 us (3%)
  between operations  14 us (2%)
    reduce_scatter x1, waiting for transfers between devices, device_step(): dx_loc = lax.psum_scatter(dx_part, 'tp', scatter_dimension=1, tiled=True)  167 us
    dot_general x1, matrix products, device_step(): jnp.einsum('hsv,hsd->vd', d_logits, x_all, preferred_element_type=jnp.flo...  105 us
    dot_general x1, matrix products, device_step(): jnp.einsum('hsv,vd->hsd', d_logits, embed, preferred_element_type=jnp.flo...  84.4 us
    dot_general x1, matrix products, device_step(): jnp.einsum('hsd,vd->hsv', x_all, embed, preferred_element_type=jnp.float32)  79.5 us
    all_gather x1, waiting for transfers between devices, device_step(): x_all = lax.all_gather(x_loc, 'tp', axis=1, tiled=True)  69.8 us
    psum x1, waiting for transfers between devices, device_step(): lax.psum((d_w_part, d_scale_part, d_shift_part), 'tp')  40.6 us
    psum x1, blocking collectives, device_step(): glob_stats = lax.psum(part_stats, 'tp')  23.9 us
    psum x1, blocking collectives, device_step(): lax.psum((d_w_part, d_scale_part, d_shift_part), 'tp')  22.6 us
  transfers between devices with their start and end apart: 3, of which 3 were waited for; matrix products, arithmetic and copies ran while one was open for 16% of the time, Pallas kernels for 0%

commit v1 on v0

v1 whole, which is shorter than its diff:
```python
import functools

import jax
import jax.numpy as jnp
from jax import lax
from jax.experimental import pallas as pl
from jax.experimental.pallas import tpu as pltpu
from jax.sharding import PartitionSpec as P

LN_EPS = 1e-5
CHIPS = 4
BLOCKS = 8
F32 = jnp.float32
BF16 = jnp.bfloat16


def to(idx):
    return dict(device_id={'tp': idx}, device_id_type=pl.DeviceIdType.MESH)


def remote(src, dst, send, recv, idx):
    return pltpu.make_async_remote_copy(src_ref=src, dst_ref=dst, send_sem=send, recv_sem=recv, **to(idx))


def stream_kernel(dims, h_ref, w_ref, gain_ref, bias_ref, e_ref, code_ref,
                  hall_ref, xall_ref, dzt_ref, dgall_ref, da1_ref, dgown_ref, loss_ref, total_ref, dgb_ref,
                  e_v, w_v, a_v, x_v, z_v, dz_v, dx_v, pr_v, mg_v, ow_v, hown_v, a2own_v, dg_v, da_v,
                  stsrc_v, strcv_v, crcv_v, tgt_v, msk_v, wgt_v, ms_v, row_v, tot_v, gsrc_v, grcv_v,
                  ld_sem, h_send, h_recv, h_loc, g_send, g_recv, g_loc,
                  st_send, st_recv, pr_send, pr_recv, r2_send, r3_send, mg_recv, ow_recv, pair_free,
                  cd_send, cd_recv, x_sem, dz_sem, a_sem, out_sem, gb_send, gb_recv):
    n, q, depth, rows, rc, nc = dims
    half = CHIPS * q
    tok = 2 * half
    cols = 2 * tok
    me = lax.axis_index('tp')
    chip = me // 2
    core = me % 2
    peer = me + 1 - 2 * core
    right_chip = (chip + 1) % CHIPS
    left_chip = (chip + CHIPS - 1) % CHIPS
    far_chip = (chip + 2) % CHIPS
    right = right_chip * 2 + core
    left = left_chip * 2 + core

    ld_e = pltpu.make_async_copy(e_ref, e_v, ld_sem.at[0])
    ld_w = pltpu.make_async_copy(w_ref, w_v, ld_sem.at[1])
    ld_h = pltpu.make_async_copy(h_ref, hown_v, ld_sem.at[2])
    ld_h.start()
    ld_w.start()
    ld_e.start()

    barrier = pltpu.get_barrier_semaphore()
    for r in range(1, n):
        pl.semaphore_signal(barrier, inc=1, **to((me + r) % n))
    pl.semaphore_wait(barrier, n - 1)

    def code_copy(r):
        return remote(code_ref, crcv_v.at[r], cd_send.at[r], cd_recv.at[r], (me + r) % n)

    for r in range(1, n):
        code_copy(r).start()

    def g1_copies(src, dst, b, send, recv):
        piece = dst.at[b, core, chip]
        return (remote(src, piece, send.at[b, 0], recv.at[b, 0], right),
                remote(src, piece, send.at[b, 1], recv.at[b, 1], left),
                remote(src, piece, send.at[b, 2], recv.at[b, 4], peer))

    def g2_copies(dst, b, send, recv):
        fl = dst.at[b, core, left_chip]
        fr = dst.at[b, core, right_chip]
        lo, hi = pl.ds(0, q // 2), pl.ds(q // 2, q // 2)
        return (remote(fl.at[lo], fl.at[lo], send.at[b, 3], recv.at[b, 2], right),
                remote(fr.at[hi], fr.at[hi], send.at[b, 4], recv.at[b, 3], left),
                remote(fl, fl, send.at[b, 5], recv.at[b, 5], peer),
                remote(fr, fr, send.at[b, 6], recv.at[b, 6], peer))

    def g3_copies(dst, b, send, recv):
        far = dst.at[b, core, far_chip]
        return (remote(far, far, send.at[b, 7], recv.at[b, 7], peer),)

    def gather1(src, dst, b, send, recv, loc):
        for c in g1_copies(src, dst, b, send, recv):
            c.start()
        pltpu.make_async_copy(src, dst.at[b, core, chip], loc.at[b]).start()

    def gather2(src, dst, b, send, recv, loc):
        c1 = g1_copies(src, dst, b, send, recv)
        remote(src, dst.at[b, core, left_chip], send.at[b, 0], recv.at[b, 0], right).wait_recv()
        remote(src, dst.at[b, core, right_chip], send.at[b, 1], recv.at[b, 1], left).wait_recv()
        for c in g2_copies(dst, b, send, recv):
            c.start()
        for c in c1:
            c.wait_send()
        pltpu.make_async_copy(src, dst.at[b, core, chip], loc.at[b]).wait()

    def gather3(dst, b, send, recv):
        far = dst.at[b, core, far_chip]
        lo, hi = pl.ds(0, q // 2), pl.ds(q // 2, q // 2)
        remote(far.at[lo], far.at[lo], send.at[b, 3], recv.at[b, 2], right).wait_recv()
        remote(far.at[hi], far.at[hi], send.at[b, 4], recv.at[b, 3], left).wait_recv()
        for c in g3_copies(dst, b, send, recv):
            c.start()
        for c in g2_copies(dst, b, send, recv):
            c.wait_send()

    def gather4(dst, b, send, recv):
        for i, c in enumerate((chip, left_chip, right_chip, far_chip)):
            piece = dst.at[b, 1 - core, c]
            remote(piece, piece, send.at[b, 7], recv.at[b, 4 + i], peer).wait_recv()
        for c in g3_copies(dst, b, send, recv):
            c.wait_send()

    def hpiece(b):
        return hown_v.at[pl.ds(b * q, q)]

    def a_copy(b, i, kk):
        return pltpu.make_async_copy(hall_ref.at[b, kk, i], a_v.at[pl.ds((kk * CHIPS + i) * q, q)],
                                     a_sem.at[kk * CHIPS + i])

    def load_block(b):
        gather4(hall_ref, b, h_send, h_recv)
        for kk in range(2):
            for i in range(CHIPS):
                a_copy(b, i, kk).start()
        for kk in range(2):
            for i in range(CHIPS):
                a_copy(b, i, kk).wait()

        def proj(i, _):
            sl = pl.ds(pl.multiple_of(i * nc, nc), nc)
            a_v[tok:, sl] = jnp.dot(a_v[:tok, :], w_v[:, sl], preferred_element_type=F32).astype(BF16)
            return 0
        lax.fori_loop(0, depth // nc, proj, 0)
        a2own_v[b % 4] = a_v[pl.ds(pl.multiple_of(tok + core * half + chip * q, q), q), :]

    def norm_rows(start, head):
        a = a_v[pl.ds(start, 16), :].astype(F32)
        mean = jnp.mean(a, axis=-1, keepdims=True)
        cent = a - mean
        var = jnp.mean(cent * cent, axis=-1, keepdims=True)
        y = cent * lax.rsqrt(var + LN_EPS) * gain_ref[pl.ds(head, 1), :] + bias_ref[pl.ds(head, 1), :]
        x_v[pl.ds(start, 16), :] = y.astype(BF16)

    npart = depth // nc
    lrows = cols // npart

    def norm_part(i):
        head = (i * lrows) // tok
        for s in range(lrows // 16):
            norm_rows(pl.multiple_of(i * lrows + s * 16, 16), head)

    def dx_part(i, slot):
        sl = pl.ds(pl.multiple_of(i * nc, nc), nc)
        val = lax.dot_general(dz_v[...], e_v[:, sl], (((0,), (0,)), ((), ())), preferred_element_type=F32)
        for h in range(2):
            for kk in range(2):
                base = h * tok + kk * half
                dx_v[slot, kk, h, :, sl] = val[base:base + half, :]

    nr = rows // rc

    def z_part(i):
        rsl = pl.ds(pl.multiple_of(i * rc, rc), rc)
        z_v[rsl, :] = lax.dot_general(e_v[rsl, :], x_v[...], (((1,), (1,)), ((), ())), preferred_element_type=F32)

    iota16 = lambda: lax.broadcasted_iota(jnp.int32, (16, cols), 0)

    def back_part(i):
        lse = row_v[0:1, :]
        w = row_v[1:2, :]
        td = tgt_v[pl.ds(8, 1), :] - i * rc - iota16()
        for s in range(rc // 16):
            sl = pl.ds(pl.multiple_of(i * rc + s * 16, 16), 16)
            p = jnp.exp(z_v[sl, :] - lse)
            d = jnp.where(td == s * 16, p - 1.0, p) * w
            dz_v[sl, :] = d.astype(BF16)

    def stat_part(i):
        base = i * rc
        m_old = ms_v[0]
        m = m_old
        for s in range(rc // 8):
            m = jnp.maximum(m, z_v[pl.ds(pl.multiple_of(base + s * 8, 8), 8), :])
        acc = ms_v[1] * jnp.exp(m_old - m)
        tl = ms_v[2]
        td = tgt_v[pl.ds(9, 1), :] - base - lax.broadcasted_iota(jnp.int32, (8, cols), 0)
        for s in range(rc // 8):
            z = z_v[pl.ds(pl.multiple_of(base + s * 8, 8), 8), :]
            acc = acc + jnp.exp(z - m)
            tl = tl + jnp.where(td == s * 8, z, 0.0)
        ms_v[0] = m
        ms_v[1] = acc
        ms_v[2] = tl

    def stat_copy(slot, r):
        return remote(stsrc_v.at[slot], strcv_v.at[slot, r], st_send.at[slot, r], st_recv.at[slot, r], (me + r) % n)

    def send_stats(b):
        slot = b % 2
        m = ms_v[0]
        top = jnp.max(m, axis=0, keepdims=True)
        stsrc_v[slot, 0:1, :] = top
        stsrc_v[slot, 1:2, :] = jnp.sum(ms_v[1] * jnp.exp(m - top), axis=0, keepdims=True)
        stsrc_v[slot, 2:3, :] = jnp.sum(ms_v[2], axis=0, keepdims=True)
        for r in range(1, n):
            stat_copy(slot, r).start()

    def join_stats(b):
        slot = b % 2
        for r in range(1, n):
            stat_copy(slot, r).wait()
        parts = [stsrc_v[slot]] + [strcv_v[slot, r] for r in range(1, n)]
        top = parts[0][0:1]
        for p in parts[1:]:
            top = jnp.maximum(top, p[0:1])
        total = jnp.zeros_like(top)
        hit = jnp.zeros_like(top)
        for p in parts:
            total = total + p[1:2] * jnp.exp(p[0:1] - top)
            hit = hit + p[2:3]
        lse = top + jnp.log(total)
        row_v[0:1, :] = lse
        row_v[1:2, :] = wgt_v[pl.ds(b, 1), :]
        tgt_v[pl.ds(8, 1), :] = tgt_v[pl.ds(b, 1), :]
        loss = (lse - hit) * msk_v[pl.ds(b, 1), :]
        loss_ref[pl.ds(b, 1), :] = loss
        tot_v[0:1, :] = tot_v[0:1, :] + loss / tot_v[1:2, :]

    def pair_copy(b):
        slot = b % 2
        return remote(dx_v.at[slot, 1 - core], pr_v.at[slot], pr_send.at[slot], pr_recv.at[slot], peer)

    def rs1(b):
        @pl.when(b >= 2)
        def _():
            pl.semaphore_wait(pair_free, 1)
        pair_copy(b).start()

    def crow(c):
        return pl.ds(pl.multiple_of(c * q, q), q)

    def r2_copies(b):
        s2, s3 = b % 2, b % 3
        mine = dx_v.at[s2, core]
        return (remote(mine.at[0, crow(far_chip)], mg_v.at[s2, 0], r2_send.at[s2, 0], mg_recv.at[s2, 0], right),
                remote(mine.at[1, crow(far_chip)], mg_v.at[s2, 1], r2_send.at[s2, 1], mg_recv.at[s2, 1], left),
                remote(mine.at[1, crow(right_chip)], ow_v.at[s3, 0, 1], r2_send.at[s2, 2], ow_recv.at[s3, 0, 1], right),
                remote(mine.at[0, crow(left_chip)], ow_v.at[s3, 1, 0], r2_send.at[s2, 3], ow_recv.at[s3, 1, 0], left))

    def rs2(b):
        slot = b % 2
        pair_copy(b).wait()

        def add(i, _):
            h = i // CHIPS
            c = i % CHIPS
            dx_v[slot, core, h, crow(c), :] += pr_v[slot, h, crow(c), :]
            return 0
        lax.fori_loop(0, 2 * CHIPS, add, 0)

        @pl.when(b < BLOCKS - 2)
        def _():
            pl.semaphore_signal(pair_free, inc=1, **to(peer))
        for c in r2_copies(b):
            c.start()

    def r3_copies(b):
        s2, s3 = b % 2, b % 3
        mine = dx_v.at[s2, core]
        return (remote(mine.at[0, crow(right_chip)], ow_v.at[s3, 0, 0], r3_send.at[s2, 0], ow_recv.at[s3, 0, 0], right),
                remote(mine.at[1, crow(left_chip)], ow_v.at[s3, 1, 1], r3_send.at[s2, 1], ow_recv.at[s3, 1, 1], left))

    def rs3(b):
        s2 = b % 2
        c2 = r2_copies(b)
        c2[0].wait_recv()
        c2[1].wait_recv()
        dx_v[s2, core, 0, crow(right_chip), :] += mg_v[s2, 0]
        dx_v[s2, core, 1, crow(left_chip), :] += mg_v[s2, 1]
        for c in r3_copies(b):
            c.start()
        for c in c2:
            c.wait_send()

    def rs4(b):
        s2, s3 = b % 2, b % 3
        c2, c3 = r2_copies(b), r3_copies(b)
        c2[2].wait_recv()
        c2[3].wait_recv()
        c3[0].wait_recv()
        c3[1].wait_recv()

        @pl.when(b >= 1)
        def _():
            out_copies(b - 1)[0].wait()
            out_copies(b - 1)[1].wait()
        for h in range(2):
            dy = dx_v[s2, core, h, crow(chip), :] + ow_v[s3, 0, h] + ow_v[s3, 1, h]
            a = (hown_v[pl.ds(pl.multiple_of(b * q, q), q), :] if h == 0 else a2own_v[b % 4]).astype(F32)
            mean = jnp.mean(a, axis=-1, keepdims=True)
            cent = a - mean
            rstd = lax.rsqrt(jnp.mean(cent * cent, axis=-1, keepdims=True) + LN_EPS)
            xhat = cent * rstd
            gsrc_v[h:h + 1, :] += jnp.sum(dy * xhat, axis=0, keepdims=True)
            gsrc_v[2 + h:3 + h, :] += jnp.sum(dy, axis=0, keepdims=True)
            dxh = dy * gain_ref[h:h + 1, :]
            c1 = jnp.mean(dxh, axis=-1, keepdims=True)
            c2_ = jnp.mean(dxh * xhat, axis=-1, keepdims=True)
            da = rstd * (dxh - c1 - xhat * c2_)
            if h == 0:
                da_v[...] = da
            else:
                dg_v[b % 4] = da.astype(BF16)
        for c in out_copies(b):
            c.start()
        for c in c3:
            c.wait_send()

    def out_copies(b):
        return (pltpu.make_async_copy(da_v, da1_ref.at[b], out_sem.at[0]),
                pltpu.make_async_copy(dg_v.at[b % 4], dgown_ref.at[b], out_sem.at[1]))

    def inside(b, fn):
        @pl.when(jnp.logical_and(b >= 0, b < BLOCKS))
        def _():
            fn(b)

    def between(j, lo, hi, fn):
        @pl.when(jnp.logical_and(j >= lo, j <= hi))
        def _():
            fn()

    def x_copy(b):
        return pltpu.make_async_copy(x_v, xall_ref.at[pl.ds(pl.multiple_of(b * cols, cols), cols)], x_sem)

    def dz_copy(b):
        return pltpu.make_async_copy(dz_v, dzt_ref.at[:, pl.ds(pl.multiple_of(b * cols, cols), cols)], dz_sem)

    def loop(k, fn):
        def body(i, _):
            fn(i)
            return 0
        lax.fori_loop(0, k, body, 0)

    ld_h.wait()
    gather1(hpiece(0), hall_ref, 0, h_send, h_recv, h_loc)
    gather1(hpiece(1), hall_ref, 1, h_send, h_recv, h_loc)
    for r in range(1, n):
        code_copy(r).wait()
    code = code_ref[...]
    for r in range(1, n):
        code = code + crcv_v[r]
    mask = (code >= 65536).astype(jnp.int32)
    tgt_v[0:BLOCKS, :] = code - mask * 65536 - me * rows
    maskf = mask.astype(F32)
    msk_v[...] = maskf
    per_col = jnp.sum(maskf, axis=0, keepdims=True)
    n0 = jnp.sum(per_col[:, :tok], axis=1, keepdims=True)
    n1 = jnp.sum(per_col[:, tok:], axis=1, keepdims=True)
    counts = jnp.concatenate([jnp.broadcast_to(n0, (1, tok)), jnp.broadcast_to(n1, (1, tok))], axis=1)
    wgt_v[...] = maskf / counts
    tot_v[0:1, :] = jnp.zeros((1, cols), F32)
    tot_v[1:2, :] = counts
    gsrc_v[...] = jnp.zeros_like(gsrc_v)
    gather2(hpiece(0), hall_ref, 0, h_send, h_recv, h_loc)
    gather3(hall_ref, 0, h_send, h_recv)
    gather2(hpiece(1), hall_ref, 1, h_send, h_recv, h_loc)
    ld_w.wait()
    load_block(0)
    ld_e.wait()

    def step(t, _):
        j = t - 1
        between(j, 1, BLOCKS, lambda: x_wait(j))

        def full_a():
            def body(i):
                dx_part(i, (j - 1) % 2)
                norm_part(i)
            loop(npart, body)
        between(j, -1, 0, lambda: loop(npart, norm_part))
        between(j, 1, BLOCKS - 2, full_a)
        between(j, BLOCKS - 1, BLOCKS, lambda: loop(npart, lambda i: dx_part(i, (j - 1) % 2)))
        inside(j - 1, rs1)
        between(j, -1, BLOCKS - 2, lambda: x_copy(j + 1).start())
        inside(j - 2, rs3)
        between(j, -1, BLOCKS - 4, lambda: gather1(hpiece(j + 3), hall_ref, j + 3, h_send, h_recv, h_loc))
        between(j, -1, BLOCKS - 3, lambda: gather3(hall_ref, j + 2, h_send, h_recv))
        inside(j - 3, lambda b: gather2(dg_v.at[b % 4], dgall_ref, b, g_send, g_recv, g_loc))
        inside(j, join_stats)
        between(j, 1, BLOCKS, lambda: dz_copy(j - 1).wait())

        def start_stats():
            ms_v[0] = jnp.full((8, cols), -3.0e38, F32)
            ms_v[1] = jnp.zeros((8, cols), F32)
            ms_v[2] = jnp.zeros((8, cols), F32)
            tgt_v[pl.ds(9, 1), :] = tgt_v[pl.ds(j + 1, 1), :]
        between(j, -1, BLOCKS - 2, start_stats)

        def full_d(i):
            back_part(i)
            z_part(i)
            stat_part(i)

        def only_z(i):
            z_part(i)
            stat_part(i)
        between(j, -1, -1, lambda: loop(nr, only_z))
        between(j, 0, BLOCKS - 2, lambda: loop(nr, full_d))
        between(j, BLOCKS - 1, BLOCKS - 1, lambda: loop(nr, back_part))
        between(j, -1, BLOCKS - 2, lambda: send_stats(j + 1))
        inside(j, lambda b: dz_copy(b).start())
        inside(j - 1, rs2)

        def finish(b):
            rs4(b)
            gather1(dg_v.at[b % 4], dgall_ref, b, g_send, g_recv, g_loc)
        inside(j - 2, finish)
        between(j, -1, BLOCKS - 4, lambda: gather2(hpiece(j + 3), hall_ref, j + 3, h_send, h_recv, h_loc))
        inside(j - 3, lambda b: gather3(dgall_ref, b, g_send, g_recv))
        between(j, -1, BLOCKS - 3, lambda: load_block(j + 2))
        return 0

    def x_wait(j):
        @pl.when(j <= BLOCKS - 1)
        def _():
            x_copy(j).wait()

    def first_x(j):
        x_copy(j).wait()

    def step_outer(t, c):
        @pl.when(t == 1)
        def _():
            first_x(0)
        return step(t, c)

    lax.fori_loop(0, BLOCKS + 4, step_outer, 0)

    for b in range(BLOCKS):
        gather4(dgall_ref, b, g_send, g_recv)
    for c in out_copies(BLOCKS - 1):
        c.wait()
    total_ref[...] = jnp.broadcast_to(jnp.sum(tot_v[0:1, :], axis=1, keepdims=True), total_ref.shape)

    def gb_copy(r):
        return remote(gsrc_v, grcv_v.at[r], gb_send.at[r], gb_recv.at[r], (me + r) % n)
    for r in range(1, n):
        gb_copy(r).start()
    for r in range(1, n):
        gb_copy(r).wait()
    acc = gsrc_v[...]
    for r in range(1, n):
        acc = acc + grcv_v[r]
    dgb_ref[...] = acc


def stream(n, hidden, w_two, gain, bias, embed, code):
    tokens, depth = hidden.shape
    rows = embed.shape[0]
    q = tokens // BLOCKS
    half = CHIPS * q
    tok = 2 * half
    cols = 2 * tok
    nc = min(512, depth // 4)
    rc = min(512, rows // 4)
    dims = (n, q, depth, rows, rc, nc)
    any_spec = pl.BlockSpec(memory_space=pl.ANY)
    vmem = pl.BlockSpec(memory_space=pltpu.VMEM)
    dma = pltpu.SemaphoreType.DMA
    sds = jax.ShapeDtypeStruct
    return pl.pallas_call(
        functools.partial(stream_kernel, dims),
        out_shape=(sds((BLOCKS, 2, CHIPS, q, depth), BF16), sds((BLOCKS * cols, depth), BF16),
                   sds((rows, BLOCKS * cols), BF16), sds((BLOCKS, 2, CHIPS, q, depth), BF16),
                   sds((BLOCKS, q, depth), F32), sds((BLOCKS, q, depth), BF16),
                   sds((BLOCKS, cols), F32), sds((8, 128), F32), sds((8, depth), F32)),
        in_specs=[any_spec, any_spec, vmem, vmem, any_spec, vmem],
        out_specs=(any_spec,) * 6 + (vmem,) * 3,
        scratch_shapes=[
            pltpu.VMEM((rows, depth), BF16), pltpu.VMEM((depth, depth), BF16),
            pltpu.VMEM((cols, depth), BF16), pltpu.VMEM((cols, depth), BF16),
            pltpu.VMEM((rows, cols), F32), pltpu.VMEM((rows, cols), BF16),
            pltpu.VMEM((2, 2, 2, half, depth), F32), pltpu.VMEM((2, 2, half, depth), F32),
            pltpu.VMEM((2, 2, q, depth), F32), pltpu.VMEM((3, 2, 2, q, depth), F32),
            pltpu.VMEM((tokens, depth), BF16), pltpu.VMEM((4, q, depth), BF16),
            pltpu.VMEM((4, q, depth), BF16), pltpu.VMEM((q, depth), F32),
            pltpu.VMEM((2, 8, cols), F32), pltpu.VMEM((2, n, 8, cols), F32),
            pltpu.VMEM((n, BLOCKS, cols), jnp.int32), pltpu.VMEM((16, cols), jnp.int32),
            pltpu.VMEM((BLOCKS, cols), F32), pltpu.VMEM((BLOCKS, cols), F32),
            pltpu.VMEM((3, 8, cols), F32), pltpu.VMEM((8, cols), F32), pltpu.VMEM((8, cols), F32),
            pltpu.VMEM((8, depth), F32), pltpu.VMEM((n, 8, depth), F32),
            dma((3,)), dma((BLOCKS, 8)), dma((BLOCKS, 8)), dma((BLOCKS,)), dma((BLOCKS, 8)), dma((BLOCKS, 8)),
            dma((BLOCKS,)), dma((2, n)), dma((2, n)), dma((2,)), dma((2,)), dma((2, 4)), dma((2, 2)),
            dma((2, 2)), dma((3, 2, 2)), pltpu.SemaphoreType.REGULAR,
            dma((n,)), dma((n,)), dma, dma, dma((8,)), dma((2,)), dma((n,)), dma((n,)),
        ],
        compiler_params=pltpu.CompilerParams(collective_id=0, has_side_effects=True, vmem_limit_bytes=67043328),
        name='stream',
    )(hidden, w_two, gain, bias, embed, code)


def solution(mesh):
    n = mesh.shape['tp']
    tok_spec = P(('dp', 'tp'), None)
    row_spec = P(None, ('dp', 'tp'))

    def device_step(hidden, w_two, ln_scale, ln_shift, embed, targets, loss_mask):
        tokens, depth = hidden.shape
        q = tokens // BLOCKS
        me = lax.axis_index('tp')
        code = (targets + 65536 * loss_mask).reshape(2, BLOCKS, q).transpose(1, 0, 2)
        place = (me % 2) * CHIPS + me // 2
        seat = lax.broadcasted_iota(jnp.int32, (1, 1, 2 * CHIPS, 1), 2) == place
        code = jnp.where(seat, code[:, :, None, :], 0).reshape(BLOCKS, 2 * 2 * CHIPS * q)
        hall, xall, dzt, dgall, da1, dgown, loss, total, dgb = stream(n, hidden, w_two, ln_scale, ln_shift, embed, code)
        d_embed = jnp.dot(dzt, xall, preferred_element_type=F32)
        d_w = lax.dot_general(hall.reshape(n * tokens, depth), dgall.reshape(n * tokens, depth),
                              (((0,), (0,)), ((), ())), preferred_element_type=F32)
        d_proj = dgown.reshape(tokens, depth)
        back = lax.dot_general(d_proj, w_two, (((1,), (1,)), ((), ())), preferred_element_type=F32)
        d_hidden = (da1.reshape(tokens, depth) + back).astype(BF16)
        loss = loss.reshape(BLOCKS, 2, 2 * CHIPS, q)
        mine = lax.dynamic_index_in_dim(loss, place, axis=2, keepdims=False)
        token_loss = mine.transpose(1, 0, 2).reshape(2, tokens)
        return token_loss, total[0, :1], d_hidden, d_embed, d_w, dgb[0:2], dgb[2:4]

    return jax.shard_map(device_step, mesh=mesh,
                         in_specs=(tok_spec, P(), P(), P(), P('tp', None), row_spec, row_spec),
                         out_specs=(row_spec, P('dp'), tok_spec, tok_spec, P('dp', None), P('dp', None), P('dp', None)),
                         check_vma=False)
```

time: 725 us -> 449 us (0.62)
  Pallas kernels: 0 us -> 334 us
  waiting for transfers between devices: 278 us -> 0 us
  matrix products: 292 us -> 108 us
  blocking collectives: 82.7 us -> 0 us
  other arithmetic: 35.3 us -> 1.32 us
  local copies, waits for them, and re-layouts: 22.9 us -> 4.54 us
  between operations: 14 us -> 0.7 us
    pallas_call x0 -> x1, Pallas kernels: none -> 334 us  [stream(): pl.pallas_call(functools.partial(stream_kernel, dims), out_shape=(sds((BL...]
    dot_general x6 -> x3, matrix products: 292 us -> 108 us  [the longest x1 78.3 us: device_step(): d_embed = jnp.dot(dzt, xall, preferred_element_type=F32)]
    reduce_scatter x1 -> x0, waiting for transfers between devices: 167 us -> none  [device_step(): dx_loc = lax.psum_scatter(dx_part, 'tp', scatter_dimension=1, tiled=True)]
    all_gather x1 -> x0, waiting for transfers between devices: 69.8 us -> none  [device_step(): x_all = lax.all_gather(x_loc, 'tp', axis=1, tiled=True)]
    psum x2 -> x0, blocking collectives: 46.6 us -> none  [the longest x1 23.9 us: device_step(): glob_stats = lax.psum(part_stats, 'tp')]
    psum x1 -> x0, waiting for transfers between devices: 40.6 us -> none  [device_step(): lax.psum((d_w_part, d_scale_part, d_shift_part), 'tp')]
    reduce_sum x7 -> x0, other arithmetic: 30.8 us -> none  [the longest x1 21.5 us: device_step(): jnp.sum(exp_loc, axis=-1) * jnp.exp(local_max - glob_max)]
    pmax x1 -> x0, blocking collectives: 21.2 us -> none  [device_step(): glob_max = lax.pmax(local_max, 'tp')]
  transfers between devices with their start and end apart: 3 -> 0, of which waited for: 3 -> 0; matrix products, arithmetic and copies ran while one was open for 16% -> 0% of each run, Pallas kernels for 0% -> 0%
where the time goes in v1:
time: 449 us
  Pallas kernels  334 us (74%)
  matrix products  108 us (24%)
  local copies, waits for them, and re-layouts  4.54 us (1%)
    pallas_call x1, Pallas kernels, stream(): pl.pallas_call(functools.partial(stream_kernel, dims), out_shape=(sds((BL...  334 us
    dot_general x1, matrix products, device_step(): d_embed = jnp.dot(dzt, xall, preferred_element_type=F32)  78.3 us
    dot_general x1, matrix products, device_step(): lax.dot_general(hall.reshape(n * tokens, depth), dgall.reshape(n * tokens...  21.9 us

profile of v1, /device:TPU:81, one launch (start us, length us, event | category | flops | bytes accessed | tf_op | source)
XLA Modules:
  0.0 448.9 jit_solution(1703493253414140479)
XLA Ops:
  0.7 0.1 broadcast_in_dim.27
  0.7 0.1 broadcast_in_dim.28
  0.8 0.7 multiply_add_fusion
  1.5 0.1 reshape.40
  1.6 0.1 broadcast_in_dim.31
  1.7 0.6 broadcast_select_fusion.code_ref
  2.3 334.3 %stream.1 = (bf16[8,2,4,32,2048]{4,3,2,1,0:T(8,128)(2,1)}, bf16[4096,2048]{1,0:T(8,128)(2,1)}, bf16[4096,4096]{1,0:T(8,128)(2,1)}, bf16[8,2,4,32,2048]{4,3,2,1,0...) custom-call(bf16[256,2048]{1,0:T(8,128)(2,1)} %h_ref.1, ...), custom_call_target="tpu_custom_call" | custom-call | tf_op jit(solution)/shard_map/stream/pallas_call | solution.py:474
  336.7 1.2 slice.9
  337.9 1.5 fusion.1
  339.4 0.8 reshape.41
  340.2 0.7 reshape.42
  340.9 0.0 copy-start
  340.9 7.8 %fusion = bf16[256,2048]{1,0:T(8,128)(2,1)} fusion(f32[256,2048]{1,0:T(8,128)} %bitcast.23, bf16[256,2048]{1,0:T(8,128)(2,1)} %bitcast.24, bf16[2048,2048]{1,0:T(8,128)(2,1)} %w_ref.1), kind=kOutput, calls=%fused_computation.2 | convolution fusion | flops 2148532224 | bytes 12582912 | tf_op jit(solution)/shard_map/dot_general | solution.py:523
  348.7 0.0 copy-done
  348.7 21.9 %convolution_bitcast_fusion = f32[2048,2048]{1,0:T(8,128)} fusion(bf16[8,2,4,32,2048]{4,3,2,1,0:T(8,128)(2,1)S(1)} %copy-done, bf16[8,2,4,32,2048]{4,3,2,1,0:T(8,128)(2,1)} %get-tuple-element.23), kind=kOutput, calls=%fused_computation | convolution fusion | flops 17179869184 | bytes 33554432 | tf_op jit(solution)/shard_map/dot_general | solution.py:520
  370.6 78.3 %fusion.2 = f32[4096,2048]{1,0:T(8,128)} fusion(bf16[4096,4096]{1,0:T(8,128)(2,1)} %get-tuple-element.20, bf16[4096,2048]{1,0:T(8,128)(2,1)} %get-tuple-element.21), kind=kOutput, calls=%fused_computation.9 | convolution fusion | flops 68719476736 | bytes 83886080 | tf_op jit(solution)/shard_map/dot_general | solution.py:519
  (5 shorter events, 0.0 us)
Async XLA Ops:
  340.9 7.8 %copy-start = (bf16[8,2,4,32,2048]{4,3,2,1,0:T(8,128)(2,1)S(1)}, bf16[8,2,4,32,2048]{4,3,2,1,0:T(8,128)(2,1)}, u32[]{:S(2)}) copy-start(bf16[8,2,4,32,2048]{4,3,2,1,0:T(8,128)(2,1)} %get-tuple-element.22) | copy-start | bytes 25165828

commit v2 on v1

--- a/solution.py
+++ b/solution.py
@@ -10,6 +10,9 @@
 LN_EPS = 1e-5
 CHIPS = 4
 BLOCKS = 8
+KEEP = 5
+WAYS = 4
+LANES = 2
 F32 = jnp.float32
 BF16 = jnp.bfloat16
 
@@ -23,13 +26,14 @@
 
 
 def stream_kernel(dims, h_ref, w_ref, gain_ref, bias_ref, e_ref, code_ref,
-                  hall_ref, xall_ref, dzt_ref, dgall_ref, da1_ref, dgown_ref, loss_ref, total_ref, dgb_ref,
+                  hall_ref, xall_ref, dzt_ref, dgall_ref, da1_ref, dgown_ref, loss_ref, total_ref, dgb_ref, de_ref,
                   e_v, w_v, a_v, x_v, z_v, dz_v, dx_v, pr_v, mg_v, ow_v, hown_v, a2own_v, dg_v, da_v,
                   stsrc_v, strcv_v, crcv_v, tgt_v, msk_v, wgt_v, ms_v, row_v, tot_v, gsrc_v, grcv_v,
                   ld_sem, h_send, h_recv, h_loc, g_send, g_recv, g_loc,
                   st_send, st_recv, pr_send, pr_recv, r2_send, r3_send, mg_recv, ow_recv, pair_free,
-                  cd_send, cd_recv, x_sem, dz_sem, a_sem, out_sem, gb_send, gb_recv):
-    n, q, depth, rows, rc, nc = dims
+                  cd_send, cd_recv, x_sem, dz_sem, a_sem, out_sem, gb_send, gb_recv, xin_sem, dzin_sem, de_sem):
+    n, q, depth, rows, rc, nc, sub = dims
+    re = rows // BLOCKS
     half = CHIPS * q
     tok = 2 * half
     cols = 2 * tok
@@ -119,11 +123,13 @@
         return pltpu.make_async_copy(hall_ref.at[b, kk, i], a_v.at[pl.ds((kk * CHIPS + i) * q, q)],
                                      a_sem.at[kk * CHIPS + i])
 
-    def load_block(b):
+    def fetch_block(b):
         gather4(hall_ref, b, h_send, h_recv)
         for kk in range(2):
             for i in range(CHIPS):
                 a_copy(b, i, kk).start()
+
+    def project_block(b):
         for kk in range(2):
             for i in range(CHIPS):
                 a_copy(b, i, kk).wait()
@@ -161,38 +167,64 @@
 
     nr = rows // rc
 
-    def z_part(i):
-        rsl = pl.ds(pl.multiple_of(i * rc, rc), rc)
-        z_v[rsl, :] = lax.dot_general(e_v[rsl, :], x_v[...], (((1,), (1,)), ((), ())), preferred_element_type=F32)
-
-    iota16 = lambda: lax.broadcasted_iota(jnp.int32, (16, cols), 0)
-
-    def back_part(i):
-        lse = row_v[0:1, :]
-        w = row_v[1:2, :]
-        td = tgt_v[pl.ds(8, 1), :] - i * rc - iota16()
-        for s in range(rc // 16):
-            sl = pl.ds(pl.multiple_of(i * rc + s * 16, 16), 16)
-            p = jnp.exp(z_v[sl, :] - lse)
-            d = jnp.where(td == s * 16, p - 1.0, p) * w
-            dz_v[sl, :] = d.astype(BF16)
-
-    def stat_part(i):
-        base = i * rc
-        m_old = ms_v[0]
-        m = m_old
-        for s in range(rc // 8):
-            m = jnp.maximum(m, z_v[pl.ds(pl.multiple_of(base + s * 8, 8), 8), :])
-        acc = ms_v[1] * jnp.exp(m_old - m)
-        tl = ms_v[2]
-        td = tgt_v[pl.ds(9, 1), :] - base - lax.broadcasted_iota(jnp.int32, (8, cols), 0)
-        for s in range(rc // 8):
-            z = z_v[pl.ds(pl.multiple_of(base + s * 8, 8), 8), :]
-            acc = acc + jnp.exp(z - m)
-            tl = tl + jnp.where(td == s * 8, z, 0.0)
-        ms_v[0] = m
-        ms_v[1] = acc
-        ms_v[2] = tl
+    def tree(parts, op):
+        while len(parts) > 1:
+            parts = [op(a, b) for a, b in zip(parts[::2], parts[1::2])]
+        return parts[0]
+
+    def part_view(ref, i):
+        return ref.at[pl.ds(pl.multiple_of(i * rc, rc), rc)]
+
+    def back_part(i, p, lanes, td):
+        shift, w = row_v[0:1, lanes], row_v[1:2, lanes]
+        zc, dc = part_view(z_v, i), part_view(dz_v, i)
+        for s in range(p * sub, p * sub + sub, 16):
+            both = []
+            for t in (s, s + 8):
+                pw = jnp.exp(zc[t:t + 8, lanes] - shift)
+                both.append(jnp.where(td == t, pw - w, pw))
+            dc[s:s + 16, lanes] = jnp.concatenate(both, axis=0).astype(BF16)
+
+    def z_part(i, p):
+        ec = part_view(e_v, i)
+        part_view(z_v, i)[p * sub:p * sub + sub, :] = lax.dot_general(
+            ec[p * sub:p * sub + sub, :], x_v[...], (((1,), (1,)), ((), ())), preferred_element_type=F32)
+
+    def stat_part(i, p, lanes, td, state):
+        zc = part_view(z_v, i)
+        m_old, acc, tl = state
+        at = range(p * sub, p * sub + sub, 8)
+        tops = [zc[s:s + 8, lanes] for s in at[:WAYS]]
+        for k, s in enumerate(at[WAYS:]):
+            tops[k % WAYS] = jnp.maximum(tops[k % WAYS], zc[s:s + 8, lanes])
+        m = jnp.maximum(m_old, tree(tops, jnp.maximum))
+        accs = [None] * WAYS
+        for k, s in enumerate(at):
+            z = zc[s:s + 8, lanes]
+            e = jnp.exp(z - m)
+            accs[k % WAYS] = e if accs[k % WAYS] is None else accs[k % WAYS] + e
+            tl = jnp.where(td == s, z, tl)
+        return m, acc * jnp.exp(m_old - m) + tree(accs, jnp.add), tl
+
+    def d_body(i, back, new):
+        span = cols // LANES
+        iota = lax.broadcasted_iota(jnp.int32, (8, span), 0)
+        cut = [slice(k * span, k * span + span) for k in range(LANES)]
+        td_old = [tgt_v[pl.ds(8, 1), c] - i * rc - iota for c in cut]
+        td_new = [tgt_v[pl.ds(9, 1), c] - i * rc - iota for c in cut]
+        state = [tuple(ms_v[k, :, c] for k in range(3)) for c in cut]
+        for p in range(rc // sub):
+            if back:
+                for k in range(LANES):
+                    back_part(i, p, cut[k], td_old[k])
+            if new:
+                z_part(i, p)
+                for k in range(LANES):
+                    state[k] = stat_part(i, p, cut[k], td_new[k], state[k])
+        if new:
+            for k in range(LANES):
+                for q_ in range(3):
+                    ms_v[q_, :, cut[k]] = state[k][q_]
 
     def stat_copy(slot, r):
         return remote(stsrc_v.at[slot], strcv_v.at[slot, r], st_send.at[slot, r], st_recv.at[slot, r], (me + r) % n)
@@ -221,8 +253,9 @@
             total = total + p[1:2] * jnp.exp(p[0:1] - top)
             hit = hit + p[2:3]
         lse = top + jnp.log(total)
-        row_v[0:1, :] = lse
-        row_v[1:2, :] = wgt_v[pl.ds(b, 1), :]
+        w = wgt_v[pl.ds(b, 1), :]
+        row_v[0:1, :] = jnp.where(w > 0.0, lse - jnp.log(jnp.where(w > 0.0, w, 1.0)), 3.0e38)
+        row_v[1:2, :] = w
         tgt_v[pl.ds(8, 1), :] = tgt_v[pl.ds(b, 1), :]
         loss = (lse - hit) * msk_v[pl.ds(b, 1), :]
         loss_ref[pl.ds(b, 1), :] = loss
@@ -281,8 +314,6 @@
         dx_v[s2, core, 1, crow(left_chip), :] += mg_v[s2, 1]
         for c in r3_copies(b):
             c.start()
-        for c in c2:
-            c.wait_send()
 
     def rs4(b):
         s2, s3 = b % 2, b % 3
@@ -315,12 +346,55 @@
                 dg_v[b % 4] = da.astype(BF16)
         for c in out_copies(b):
             c.start()
-        for c in c3:
+        for c in c2 + c3:
             c.wait_send()
 
     def out_copies(b):
         return (pltpu.make_async_copy(da_v, da1_ref.at[b], out_sem.at[0]),
                 pltpu.make_async_copy(dg_v.at[b % 4], dgown_ref.at[b], out_sem.at[1]))
+
+    def xin_copy(i):
+        sl = pl.ds(pl.multiple_of(i * nc, nc), nc)
+        return pltpu.make_async_copy(xall_ref.at[:, sl], e_v.at[:, sl], xin_sem.at[i])
+
+    def dzin_copy(c, hf):
+        return pltpu.make_async_copy(
+            dzt_ref.at[pl.ds(pl.multiple_of(c * re, re), re), pl.ds(hf * depth, depth)],
+            w_v.at[pl.ds(pl.multiple_of((c % 2) * 2 * re + hf * re, re), re)], dzin_sem.at[c % 2, hf])
+
+    def de_copy(c, i):
+        return pltpu.make_async_copy(
+            z_v.at[pl.ds(pl.multiple_of(i * re, re), re)],
+            de_ref.at[pl.ds(pl.multiple_of(c * re, re), re), pl.ds(pl.multiple_of(i * nc, nc), nc)], de_sem.at[i])
+
+    def de_chunk(c):
+        for hf in range(2):
+            dzin_copy(c, hf).wait()
+        base = (c % 2) * 2 * re
+        lo = w_v.at[pl.ds(pl.multiple_of(base, re), re)]
+        hi = w_v.at[pl.ds(pl.multiple_of(base + re, re), re)]
+
+        def part(i, _):
+            sl = pl.ds(pl.multiple_of(i * nc, nc), nc)
+
+            @pl.when(c == 0)
+            def _():
+                xin_copy(i).wait()
+
+            @pl.when(c >= 1)
+            def _():
+                de_copy(c - 1, i).wait()
+            val = jnp.dot(lo[...], e_v[:depth, sl], preferred_element_type=F32)
+            val = val + jnp.dot(hi[...], e_v[depth:, sl], preferred_element_type=F32)
+            z_v[pl.ds(pl.multiple_of(i * re, re), re), :] = val
+            de_copy(c, i).start()
+            return 0
+        lax.fori_loop(0, npart, part, 0)
+
+        @pl.when(c + 2 < KEEP)
+        def _():
+            for hf in range(2):
+                dzin_copy(c + 2, hf).start()
 
     def inside(b, fn):
         @pl.when(jnp.logical_and(b >= 0, b < BLOCKS))
@@ -353,7 +427,8 @@
     for r in range(1, n):
         code = code + crcv_v[r]
     mask = (code >= 65536).astype(jnp.int32)
-    tgt_v[0:BLOCKS, :] = code - mask * 65536 - me * rows
+    local = code - mask * 65536 - me * rows
+    tgt_v[0:BLOCKS, :] = jnp.where(jnp.logical_and(local >= 0, local < rows), local, -(1 << 24))
     maskf = mask.astype(F32)
     msk_v[...] = maskf
     per_col = jnp.sum(maskf, axis=0, keepdims=True)
@@ -368,7 +443,8 @@
     gather3(hall_ref, 0, h_send, h_recv)
     gather2(hpiece(1), hall_ref, 1, h_send, h_recv, h_loc)
     ld_w.wait()
-    load_block(0)
+    fetch_block(0)
+    project_block(0)
     ld_e.wait()
 
     def step(t, _):
@@ -382,15 +458,26 @@
             loop(npart, body)
         between(j, -1, 0, lambda: loop(npart, norm_part))
         between(j, 1, BLOCKS - 2, full_a)
-        between(j, BLOCKS - 1, BLOCKS, lambda: loop(npart, lambda i: dx_part(i, (j - 1) % 2)))
+        between(j, BLOCKS, BLOCKS, start_tail)
+
+        def last_a(i):
+            dx_part(i, (j - 1) % 2)
+
+            @pl.when(j == BLOCKS)
+            def _():
+                xin_copy(i).start()
+        between(j, BLOCKS - 1, BLOCKS, lambda: loop(npart, last_a))
+        between(j, BLOCKS + 1, BLOCKS + 2, lambda: de_chunk(2 * (j - BLOCKS) - 1))
         inside(j - 1, rs1)
         between(j, -1, BLOCKS - 2, lambda: x_copy(j + 1).start())
         inside(j - 2, rs3)
         between(j, -1, BLOCKS - 4, lambda: gather1(hpiece(j + 3), hall_ref, j + 3, h_send, h_recv, h_loc))
         between(j, -1, BLOCKS - 3, lambda: gather3(hall_ref, j + 2, h_send, h_recv))
         inside(j - 3, lambda b: gather2(dg_v.at[b % 4], dgall_ref, b, g_send, g_recv, g_loc))
+        between(j, BLOCKS + 2, BLOCKS + 2, gb_start)
         inside(j, join_stats)
-        between(j, 1, BLOCKS, lambda: dz_copy(j - 1).wait())
+        between(j, 1, BLOCKS - 1, lambda: dz_copy(j - 1).wait())
+        between(j, BLOCKS, BLOCKS + 2, lambda: de_chunk(2 * (j - BLOCKS)))
 
         def start_stats():
             ms_v[0] = jnp.full((8, cols), -3.0e38, F32)
@@ -399,18 +486,11 @@
             tgt_v[pl.ds(9, 1), :] = tgt_v[pl.ds(j + 1, 1), :]
         between(j, -1, BLOCKS - 2, start_stats)
 
-        def full_d(i):
-            back_part(i)
-            z_part(i)
-            stat_part(i)
-
-        def only_z(i):
-            z_part(i)
-            stat_part(i)
-        between(j, -1, -1, lambda: loop(nr, only_z))
-        between(j, 0, BLOCKS - 2, lambda: loop(nr, full_d))
-        between(j, BLOCKS - 1, BLOCKS - 1, lambda: loop(nr, back_part))
+        between(j, -1, -1, lambda: loop(nr, lambda i: d_body(i, False, True)))
+        between(j, 0, BLOCKS - 2, lambda: loop(nr, lambda i: d_body(i, True, True)))
+        between(j, BLOCKS - 1, BLOCKS - 1, lambda: loop(nr, lambda i: d_body(i, True, False)))
         between(j, -1, BLOCKS - 2, lambda: send_stats(j + 1))
+        between(j, -1, BLOCKS - 3, lambda: fetch_block(j + 2))
         inside(j, lambda b: dz_copy(b).start())
         inside(j - 1, rs2)
 
@@ -420,8 +500,21 @@
         inside(j - 2, finish)
         between(j, -1, BLOCKS - 4, lambda: gather2(hpiece(j + 3), hall_ref, j + 3, h_send, h_recv, h_loc))
         inside(j - 3, lambda b: gather3(dgall_ref, b, g_send, g_recv))
-        between(j, -1, BLOCKS - 3, lambda: load_block(j + 2))
+        between(j, -1, BLOCKS - 3, lambda: project_block(j + 2))
         return 0
+
+    def gb_copy(r):
+        return remote(gsrc_v, grcv_v.at[r], gb_send.at[r], gb_recv.at[r], (me + r) % n)
+
+    def gb_start():
+        for r in range(1, n):
+            gb_copy(r).start()
+
+    def start_tail():
+        dz_copy(BLOCKS - 1).wait()
+        for c in range(2):
+            for hf in range(2):
+                dzin_copy(c, hf).start()
 
     def x_wait(j):
         @pl.when(j <= BLOCKS - 1)
@@ -445,10 +538,8 @@
         c.wait()
     total_ref[...] = jnp.broadcast_to(jnp.sum(tot_v[0:1, :], axis=1, keepdims=True), total_ref.shape)
 
-    def gb_copy(r):
-        return remote(gsrc_v, grcv_v.at[r], gb_send.at[r], gb_recv.at[r], (me + r) % n)
-    for r in range(1, n):
-        gb_copy(r).start()
+    for i in range(npart):
+        de_copy(KEEP - 1, i).wait()
     for r in range(1, n):
         gb_copy(r).wait()
     acc = gsrc_v[...]
@@ -464,9 +555,10 @@
     half = CHIPS * q
     tok = 2 * half
     cols = 2 * tok
-    nc = min(512, depth // 4)
-    rc = min(512, rows // 4)
-    dims = (n, q, depth, rows, rc, nc)
+    nc = depth // 4
+    rc, sub = rows // 2, rows // 8
+    assert BLOCKS * cols == rows == 2 * depth and nc == cols
+    dims = (n, q, depth, rows, rc, nc, sub)
     any_spec = pl.BlockSpec(memory_space=pl.ANY)
     vmem = pl.BlockSpec(memory_space=pltpu.VMEM)
     dma = pltpu.SemaphoreType.DMA
@@ -476,9 +568,10 @@
         out_shape=(sds((BLOCKS, 2, CHIPS, q, depth), BF16), sds((BLOCKS * cols, depth), BF16),
                    sds((rows, BLOCKS * cols), BF16), sds((BLOCKS, 2, CHIPS, q, depth), BF16),
                    sds((BLOCKS, q, depth), F32), sds((BLOCKS, q, depth), BF16),
-                   sds((BLOCKS, cols), F32), sds((8, 128), F32), sds((8, depth), F32)),
+                   sds((BLOCKS, cols), F32), sds((8, 128), F32), sds((8, depth), F32),
+                   sds((KEEP * (rows // BLOCKS), depth), F32)),
         in_specs=[any_spec, any_spec, vmem, vmem, any_spec, vmem],
-        out_specs=(any_spec,) * 6 + (vmem,) * 3,
+        out_specs=(any_spec,) * 6 + (vmem,) * 3 + (any_spec,),
         scratch_shapes=[
             pltpu.VMEM((rows, depth), BF16), pltpu.VMEM((depth, depth), BF16),
             pltpu.VMEM((cols, depth), BF16), pltpu.VMEM((cols, depth), BF16),
@@ -496,10 +589,68 @@
             dma((BLOCKS,)), dma((2, n)), dma((2, n)), dma((2,)), dma((2,)), dma((2, 4)), dma((2, 2)),
             dma((2, 2)), dma((3, 2, 2)), pltpu.SemaphoreType.REGULAR,
             dma((n,)), dma((n,)), dma, dma, dma((8,)), dma((2,)), dma((n,)), dma((n,)),
+            dma((depth // nc,)), dma((2, 2)), dma((depth // nc,)),
         ],
         compiler_params=pltpu.CompilerParams(collective_id=0, has_side_effects=True, vmem_limit_bytes=67043328),
         name='stream',
     )(hidden, w_two, gain, bias, embed, code)
+
+
+def dense_kernel(part_ref, dz_ref, x_ref, h_ref, g_ref, da_ref, go_ref, w_ref, de_ref, dw_ref, dh_ref, x_v, x_sem):
+    i = pl.program_id(0)
+    depth = x_v.shape[1]
+    nc = depth // 4
+    load = pltpu.make_async_copy(x_ref, x_v, x_sem)
+
+    @pl.when(i == 0)
+    def _():
+        load.start()
+
+    @pl.when(i < KEEP)
+    def _():
+        de_ref[...] = part_ref[...]
+
+    @pl.when(i == KEEP)
+    def _():
+        load.wait()
+
+    @pl.when(i >= KEEP)
+    def _():
+        def part(p, _):
+            sl = pl.ds(pl.multiple_of(p * nc, nc), nc)
+            de_ref[:, sl] = jnp.dot(dz_ref[...], x_v[:, sl], preferred_element_type=F32)
+            return 0
+        lax.fori_loop(0, 4, part, 0)
+    dw_ref[...] = lax.dot_general(h_ref[...], g_ref[...], (((0,), (0,)), ((), ())), preferred_element_type=F32)
+    back = lax.dot_general(go_ref[...], w_ref[...], (((1,), (1,)), ((), ())), preferred_element_type=F32)
+    dh_ref[...] = (da_ref[...] + back).astype(BF16)
+
+
+def dense(part, dzt, xall, hall, dgall, da1, dgown, w_two):
+    rows, kk = dzt.shape
+    depth = xall.shape[1]
+    total, tokens = hall.shape[0], da1.shape[0]
+    re, wb = rows // BLOCKS, depth // BLOCKS
+    sds = jax.ShapeDtypeStruct
+    one = pl.Buffered(buffer_count=1)
+    return pl.pallas_call(
+        dense_kernel,
+        grid=(BLOCKS,),
+        out_shape=(sds((rows, depth), F32), sds((depth, depth), F32), sds((tokens, depth), BF16)),
+        in_specs=[pl.BlockSpec((re, depth), lambda i: (jnp.minimum(i, KEEP - 1), 0)),
+                  pl.BlockSpec((re, kk), lambda i: (jnp.maximum(i, KEEP), 0)),
+                  pl.BlockSpec(memory_space=pl.ANY),
+                  pl.BlockSpec((total, wb), lambda i: (0, i)),
+                  pl.BlockSpec((total, depth), lambda i: (0, 0), pipeline_mode=one),
+                  pl.BlockSpec((tokens, wb), lambda i: (0, i)),
+                  pl.BlockSpec((tokens, depth), lambda i: (0, 0), pipeline_mode=one),
+                  pl.BlockSpec((wb, depth), lambda i: (i, 0))],
+        out_specs=(pl.BlockSpec((re, depth), lambda i: (i, 0)), pl.BlockSpec((wb, depth), lambda i: (i, 0)),
+                   pl.BlockSpec((tokens, wb), lambda i: (0, i))),
+        scratch_shapes=[pltpu.VMEM((kk, depth), BF16), pltpu.SemaphoreType.DMA],
+        compiler_params=pltpu.CompilerParams(vmem_limit_bytes=67043328),
+        name='dense',
+    )(part, dzt, xall, hall, dgall, da1, dgown, w_two)
 
 
 def solution(mesh):
@@ -515,13 +666,10 @@
         place = (me % 2) * CHIPS + me // 2
         seat = lax.broadcasted_iota(jnp.int32, (1, 1, 2 * CHIPS, 1), 2) == place
         code = jnp.where(seat, code[:, :, None, :], 0).reshape(BLOCKS, 2 * 2 * CHIPS * q)
-        hall, xall, dzt, dgall, da1, dgown, loss, total, dgb = stream(n, hidden, w_two, ln_scale, ln_shift, embed, code)
-        d_embed = jnp.dot(dzt, xall, preferred_element_type=F32)
-        d_w = lax.dot_general(hall.reshape(n * tokens, depth), dgall.reshape(n * tokens, depth),
-                              (((0,), (0,)), ((), ())), preferred_element_type=F32)
-        d_proj = dgown.reshape(tokens, depth)
-        back = lax.dot_general(d_proj, w_two, (((1,), (1,)), ((), ())), preferred_element_type=F32)
-        d_hidden = (da1.reshape(tokens, depth) + back).astype(BF16)
+        hall, xall, dzt, dgall, da1, dgown, loss, total, dgb, part = stream(
+            n, hidden, w_two, ln_scale, ln_shift, embed, code)
+        d_embed, d_w, d_hidden = dense(part, dzt, xall, hall.reshape(n * tokens, depth), dgall.reshape(n * tokens, depth),
+                                       da1.reshape(tokens, depth), dgown.reshape(tokens, depth), w_two)
         loss = loss.reshape(BLOCKS, 2, 2 * CHIPS, q)
         mine = lax.dynamic_index_in_dim(loss, place, axis=2, keepdims=False)
         token_loss = mine.transpose(1, 0, 2).reshape(2, tokens)

time: 449 us -> 396 us (0.88)
  matrix products: 108 us -> 0 us
  Pallas kernels: 334 us -> 389 us
    dot_general x3 -> x0, matrix products: 108 us -> none  [the longest x1 78.3 us: device_step(): d_embed = jnp.dot(dzt, xall, preferred_element_type=F32)]
    pallas_call x0 -> x1, Pallas kernels: none -> 69.3 us  [dense(): pl.pallas_call(dense_kernel, grid=(BLOCKS,), out_shape=(sds((rows, depth)...]
    pallas_call x1, Pallas kernels: 334 us -> 319 us  [stream(): pl.pallas_call(functools.partial(stream_kernel, dims), out_shape=(sds((BL...]
where the time goes in v2:
time: 396 us; the launch traced here: 395 us
  Pallas kernels  389 us (98%)
  local copies, waits for them, and re-layouts  4.54 us (1%)
    pallas_call x1, Pallas kernels, stream(): pl.pallas_call(functools.partial(stream_kernel, dims), out_shape=(sds((BL...  319 us
    pallas_call x1, Pallas kernels, dense(): pl.pallas_call(dense_kernel, grid=(BLOCKS,), out_shape=(sds((rows, depth)...  69.3 us

profile of v2, /device:TPU:81, one launch (start us, length us, event | category | flops | bytes accessed | tf_op | source)
XLA Modules:
  0.0 395.3 jit_solution(5062166331263732434)
XLA Ops:
  0.7 0.1 broadcast_in_dim.27
  0.7 0.1 broadcast_in_dim.28
  0.8 0.7 multiply_add_fusion
  1.5 0.1 reshape.44
  1.6 0.1 broadcast_in_dim.31
  1.7 0.6 broadcast_select_fusion.code_ref
  2.3 319.2 %stream.1 = (bf16[8,2,4,32,2048]{4,3,2,1,0:T(8,128)(2,1)}, bf16[4096,2048]{1,0:T(8,128)(2,1)}, bf16[4096,4096]{1,0:T(8,128)(2,1)}, bf16[8,2,4,32,2048]{4,3,2,1,0...) custom-call(bf16[256,2048]{1,0:T(8,128)(2,1)} %h_ref.1, ...), custom_call_target="tpu_custom_call" | custom-call | tf_op jit(solution)/shard_map/stream/pallas_call | solution.py:566
  321.6 1.2 slice.9
  322.8 1.5 fusion
  324.3 0.8 reshape.45
  325.1 0.7 reshape.46
  325.8 69.3 %dense.1 = (f32[4096,2048]{1,0:T(8,128)}, f32[2048,2048]{1,0:T(8,128)}, bf16[256,2048]{1,0:T(8,128)(2,1)}) custom-call(f32[2560,2048]{1,0:T(8,128)} %get-tuple-element.22.part_ref, bf16[4096,4096]{1,0:T(8,128)(2,1)} %get-tuple-element.23.dz_ref, bf16[4096,2048]{1,0:T(8,128)(2,1)} %get-tuple-element.24.x_ref, bf16[2048,2048]{1,0:T(8,128)(2,1)} %bitcast.13, ...), custom_call_target="tpu_custom_call" | custom-call | tf_op jit(solution)/shard_map/dense/pallas_call | solution.py:636
  (5 shorter events, 0.0 us)

commit v3 on v2

--- a/solution.py
+++ b/solution.py
@@ -26,7 +26,7 @@
 
 
 def stream_kernel(dims, h_ref, w_ref, gain_ref, bias_ref, e_ref, code_ref,
-                  hall_ref, xall_ref, dzt_ref, dgall_ref, da1_ref, dgown_ref, loss_ref, total_ref, dgb_ref, de_ref,
+                  aall_ref, xall_ref, dzt_ref, dgall_ref, da1_ref, dgown_ref, loss_ref, total_ref, dgb_ref, de_ref,
                   e_v, w_v, a_v, x_v, z_v, dz_v, dx_v, pr_v, mg_v, ow_v, hown_v, a2own_v, dg_v, da_v,
                   stsrc_v, strcv_v, crcv_v, tgt_v, msk_v, wgt_v, ms_v, row_v, tot_v, gsrc_v, grcv_v,
                   ld_sem, h_send, h_recv, h_loc, g_send, g_recv, g_loc,
@@ -65,81 +65,95 @@
     for r in range(1, n):
         code_copy(r).start()
 
-    def g1_copies(src, dst, b, send, recv):
-        piece = dst.at[b, core, chip]
-        return (remote(src, piece, send.at[b, 0], recv.at[b, 0], right),
-                remote(src, piece, send.at[b, 1], recv.at[b, 1], left),
-                remote(src, piece, send.at[b, 2], recv.at[b, 4], peer))
-
-    def g2_copies(dst, b, send, recv):
-        fl = dst.at[b, core, left_chip]
-        fr = dst.at[b, core, right_chip]
-        lo, hi = pl.ds(0, q // 2), pl.ds(q // 2, q // 2)
-        return (remote(fl.at[lo], fl.at[lo], send.at[b, 3], recv.at[b, 2], right),
-                remote(fr.at[hi], fr.at[hi], send.at[b, 4], recv.at[b, 3], left),
-                remote(fl, fl, send.at[b, 5], recv.at[b, 5], peer),
-                remote(fr, fr, send.at[b, 6], recv.at[b, 6], peer))
-
-    def g3_copies(dst, b, send, recv):
-        far = dst.at[b, core, far_chip]
-        return (remote(far, far, send.at[b, 7], recv.at[b, 7], peer),)
-
-    def gather1(src, dst, b, send, recv, loc):
-        for c in g1_copies(src, dst, b, send, recv):
+    lo, hi = pl.ds(0, q // 2), pl.ds(q // 2, q // 2)
+
+    def g1_copies(src, dst, send, recv):
+        piece = dst.at[core, chip]
+        return (remote(src, piece, send.at[0], recv.at[0], right),
+                remote(src, piece, send.at[1], recv.at[1], left),
+                remote(src, piece, send.at[2], recv.at[4], peer))
+
+    def g2_copies(dst, send, recv):
+        fl, fr = dst.at[core, left_chip], dst.at[core, right_chip]
+        return (remote(fl.at[lo], fl.at[lo], send.at[3], recv.at[2], right),
+                remote(fr.at[hi], fr.at[hi], send.at[4], recv.at[3], left),
+                remote(fl, fl, send.at[5], recv.at[5], peer),
+                remote(fr, fr, send.at[6], recv.at[6], peer))
+
+    def g3_copies(dst, send, recv):
+        far = dst.at[core, far_chip]
+        return (remote(far, far, send.at[7], recv.at[7], peer),)
+
+    def gather1(src, dst, send, recv, loc):
+        for c in g1_copies(src, dst, send, recv):
             c.start()
-        pltpu.make_async_copy(src, dst.at[b, core, chip], loc.at[b]).start()
-
-    def gather2(src, dst, b, send, recv, loc):
-        c1 = g1_copies(src, dst, b, send, recv)
-        remote(src, dst.at[b, core, left_chip], send.at[b, 0], recv.at[b, 0], right).wait_recv()
-        remote(src, dst.at[b, core, right_chip], send.at[b, 1], recv.at[b, 1], left).wait_recv()
-        for c in g2_copies(dst, b, send, recv):
+        pltpu.make_async_copy(src, dst.at[core, chip], loc).start()
+
+    def gather2(src, dst, send, recv, loc):
+        remote(src, dst.at[core, left_chip], send.at[0], recv.at[0], right).wait_recv()
+        remote(src, dst.at[core, right_chip], send.at[1], recv.at[1], left).wait_recv()
+        for c in g2_copies(dst, send, recv):
             c.start()
-        for c in c1:
+        for c in g1_copies(src, dst, send, recv):
             c.wait_send()
-        pltpu.make_async_copy(src, dst.at[b, core, chip], loc.at[b]).wait()
-
-    def gather3(dst, b, send, recv):
-        far = dst.at[b, core, far_chip]
-        lo, hi = pl.ds(0, q // 2), pl.ds(q // 2, q // 2)
-        remote(far.at[lo], far.at[lo], send.at[b, 3], recv.at[b, 2], right).wait_recv()
-        remote(far.at[hi], far.at[hi], send.at[b, 4], recv.at[b, 3], left).wait_recv()
-        for c in g3_copies(dst, b, send, recv):
+        pltpu.make_async_copy(src, dst.at[core, chip], loc).wait()
+
+    def gather3(dst, send, recv):
+        far = dst.at[core, far_chip]
+        remote(far.at[lo], far.at[lo], send.at[3], recv.at[2], right).wait_recv()
+        remote(far.at[hi], far.at[hi], send.at[4], recv.at[3], left).wait_recv()
+        for c in g3_copies(dst, send, recv):
             c.start()
-        for c in g2_copies(dst, b, send, recv):
+        for c in g2_copies(dst, send, recv):
             c.wait_send()
 
-    def gather4(dst, b, send, recv):
+    def gather4(dst, send, recv):
         for i, c in enumerate((chip, left_chip, right_chip, far_chip)):
-            piece = dst.at[b, 1 - core, c]
-            remote(piece, piece, send.at[b, 7], recv.at[b, 4 + i], peer).wait_recv()
-        for c in g3_copies(dst, b, send, recv):
+            piece = dst.at[1 - core, c]
+            remote(piece, piece, send.at[7], recv.at[4 + i], peer).wait_recv()
+        for c in g3_copies(dst, send, recv):
             c.wait_send()
 
-    def hpiece(b):
-        return hown_v.at[pl.ds(b * q, q)]
-
-    def a_copy(b, i, kk):
-        return pltpu.make_async_copy(hall_ref.at[b, kk, i], a_v.at[pl.ds((kk * CHIPS + i) * q, q)],
-                                     a_sem.at[kk * CHIPS + i])
+    def own(b, h):
+        return (hown_v if h == 0 else a2own_v).at[pl.ds(pl.multiple_of(b * q, q), q)]
+
+    def in1(b, h):
+        gather1(own(b, h), aall_ref.at[b, h], h_send.at[b, h], h_recv.at[b, h], h_loc.at[b, h])
+
+    def in2(b, h):
+        gather2(own(b, h), aall_ref.at[b, h], h_send.at[b, h], h_recv.at[b, h], h_loc.at[b, h])
+
+    def in3(b, h):
+        gather3(aall_ref.at[b, h], h_send.at[b, h], h_recv.at[b, h])
+
+    def dg1(b):
+        gather1(dg_v.at[b % 4], dgall_ref.at[b], g_send.at[b], g_recv.at[b], g_loc.at[b])
+
+    def dg2(b):
+        gather2(dg_v.at[b % 4], dgall_ref.at[b], g_send.at[b], g_recv.at[b], g_loc.at[b])
+
+    def dg3(b):
+        gather3(dgall_ref.at[b], g_send.at[b], g_recv.at[b])
+
+    def a_copy(b, h, kk, c):
+        at = pl.ds(((h * 2 + kk) * CHIPS + c) * q, q)
+        return pltpu.make_async_copy(aall_ref.at[b, h, kk, c], a_v.at[at], a_sem.at[(h * 2 + kk) * CHIPS + c])
+
+    def block_copies(b):
+        return [a_copy(b, h, kk, c) for h in range(2) for kk in range(2) for c in range(CHIPS)]
 
     def fetch_block(b):
-        gather4(hall_ref, b, h_send, h_recv)
-        for kk in range(2):
-            for i in range(CHIPS):
-                a_copy(b, i, kk).start()
-
-    def project_block(b):
-        for kk in range(2):
-            for i in range(CHIPS):
-                a_copy(b, i, kk).wait()
-
+        for h in range(2):
+            gather4(aall_ref.at[b, h], h_send.at[b, h], h_recv.at[b, h])
+        for c in block_copies(b):
+            c.start()
+
+    def project_own():
         def proj(i, _):
             sl = pl.ds(pl.multiple_of(i * nc, nc), nc)
-            a_v[tok:, sl] = jnp.dot(a_v[:tok, :], w_v[:, sl], preferred_element_type=F32).astype(BF16)
+            a2own_v[:, sl] = jnp.dot(hown_v[...], w_v[:, sl], preferred_element_type=F32).astype(BF16)
             return 0
         lax.fori_loop(0, depth // nc, proj, 0)
-        a2own_v[b % 4] = a_v[pl.ds(pl.multiple_of(tok + core * half + chip * q, q), q), :]
 
     def norm_rows(start, head):
         a = a_v[pl.ds(start, 16), :].astype(F32)
@@ -329,7 +343,7 @@
             out_copies(b - 1)[1].wait()
         for h in range(2):
             dy = dx_v[s2, core, h, crow(chip), :] + ow_v[s3, 0, h] + ow_v[s3, 1, h]
-            a = (hown_v[pl.ds(pl.multiple_of(b * q, q), q), :] if h == 0 else a2own_v[b % 4]).astype(F32)
+            a = own(b, h)[...].astype(F32)
             mean = jnp.mean(a, axis=-1, keepdims=True)
             cent = a - mean
             rstd = lax.rsqrt(jnp.mean(cent * cent, axis=-1, keepdims=True) + LN_EPS)
@@ -396,15 +410,17 @@
             for hf in range(2):
                 dzin_copy(c + 2, hf).start()
 
-    def inside(b, fn):
+    def inside(b, fn, name='svc'):
         @pl.when(jnp.logical_and(b >= 0, b < BLOCKS))
         def _():
-            fn(b)
-
-    def between(j, lo, hi, fn):
+            with jax.named_scope(name):
+                fn(b)
+
+    def between(j, lo, hi, fn, name='svc'):
         @pl.when(jnp.logical_and(j >= lo, j <= hi))
         def _():
-            fn()
+            with jax.named_scope(name):
+                fn()
 
     def x_copy(b):
         return pltpu.make_async_copy(x_v, xall_ref.at[pl.ds(pl.multiple_of(b * cols, cols), cols)], x_sem)
@@ -419,8 +435,14 @@
         lax.fori_loop(0, k, body, 0)
 
     ld_h.wait()
-    gather1(hpiece(0), hall_ref, 0, h_send, h_recv, h_loc)
-    gather1(hpiece(1), hall_ref, 1, h_send, h_recv, h_loc)
+    in1(0, 0)
+    in1(1, 0)
+    ld_w.wait()
+    project_own()
+    in1(0, 1)
+    in1(1, 1)
+    in2(0, 0)
+    in2(1, 0)
     for r in range(1, n):
         code_copy(r).wait()
     code = code_ref[...]
@@ -439,26 +461,44 @@
     tot_v[0:1, :] = jnp.zeros((1, cols), F32)
     tot_v[1:2, :] = counts
     gsrc_v[...] = jnp.zeros_like(gsrc_v)
-    gather2(hpiece(0), hall_ref, 0, h_send, h_recv, h_loc)
-    gather3(hall_ref, 0, h_send, h_recv)
-    gather2(hpiece(1), hall_ref, 1, h_send, h_recv, h_loc)
-    ld_w.wait()
+    in3(0, 0)
+    in2(0, 1)
+    in3(0, 1)
+    in2(1, 1)
     fetch_block(0)
-    project_block(0)
     ld_e.wait()
+
+    def both(fn):
+        def run(b):
+            fn(b, 0)
+            fn(b, 1)
+        return run
+
+    def last_stage(b):
+        rs4(b)
+        dg1(b)
+
+    def gather_in(h):
+        between(h, -2, BLOCKS - 5, lambda: both(in1)(h + 4), 'in1')
+        between(h, -1, BLOCKS - 4, lambda: both(in2)(h + 3), 'in2')
+        between(h, 0, BLOCKS - 3, lambda: both(in3)(h + 2), 'in3')
 
     def step(t, _):
         j = t - 1
-        between(j, 1, BLOCKS, lambda: x_wait(j))
+        def block_wait():
+            for c in block_copies(j + 1):
+                c.wait()
+        between(j, -1, BLOCKS - 2, block_wait, 'bwait')
+        between(j, 1, BLOCKS, lambda: x_wait(j), 'xwait')
 
         def full_a():
             def body(i):
                 dx_part(i, (j - 1) % 2)
                 norm_part(i)
             loop(npart, body)
-        between(j, -1, 0, lambda: loop(npart, norm_part))
-        between(j, 1, BLOCKS - 2, full_a)
-        between(j, BLOCKS, BLOCKS, start_tail)
+        between(j, -1, 0, lambda: loop(npart, norm_part), 'norm')
+        between(j, 1, BLOCKS - 2, full_a, 'full_a')
+        between(j, BLOCKS, BLOCKS, start_tail, 'start_tail')
 
         def last_a(i):
             dx_part(i, (j - 1) % 2)
@@ -466,18 +506,23 @@
             @pl.when(j == BLOCKS)
             def _():
                 xin_copy(i).start()
-        between(j, BLOCKS - 1, BLOCKS, lambda: loop(npart, last_a))
-        between(j, BLOCKS + 1, BLOCKS + 2, lambda: de_chunk(2 * (j - BLOCKS) - 1))
-        inside(j - 1, rs1)
-        between(j, -1, BLOCKS - 2, lambda: x_copy(j + 1).start())
-        inside(j - 2, rs3)
-        between(j, -1, BLOCKS - 4, lambda: gather1(hpiece(j + 3), hall_ref, j + 3, h_send, h_recv, h_loc))
-        between(j, -1, BLOCKS - 3, lambda: gather3(hall_ref, j + 2, h_send, h_recv))
-        inside(j - 3, lambda b: gather2(dg_v.at[b % 4], dgall_ref, b, g_send, g_recv, g_loc))
-        between(j, BLOCKS + 2, BLOCKS + 2, gb_start)
-        inside(j, join_stats)
-        between(j, 1, BLOCKS - 1, lambda: dz_copy(j - 1).wait())
-        between(j, BLOCKS, BLOCKS + 2, lambda: de_chunk(2 * (j - BLOCKS)))
+
+            @pl.when(jnp.logical_and(j == BLOCKS - 1, i == npart - 2))
+            def _():
+                rs3(BLOCKS - 3)
+        between(j, BLOCKS - 1, BLOCKS, lambda: loop(npart, last_a), 'last_a')
+        between(j, BLOCKS + 1, BLOCKS + 2, lambda: de_chunk(2 * (j - BLOCKS) - 1), 'de_a')
+        between(j, -1, BLOCKS - 2, lambda: x_copy(j + 1).start(), 'xstart')
+        inside(j - 1, rs1, 'rs1')
+        between(j, 2, BLOCKS - 2, lambda: rs3(j - 2), 'rs3')
+        between(j, BLOCKS, BLOCKS + 1, lambda: rs3(j - 2), 'rs3')
+        between(j, -1, -1, lambda: both(in3)(1), 'in3p')
+        gather_in(2 * j)
+        inside(j - 3, dg2, 'dg2')
+        between(j, BLOCKS + 2, BLOCKS + 2, gb_start, 'gbstart')
+        inside(j, join_stats, 'join')
+        between(j, 1, BLOCKS - 1, lambda: dz_copy(j - 1).wait(), 'dzwait')
+        between(j, BLOCKS, BLOCKS + 2, lambda: de_chunk(2 * (j - BLOCKS)), 'de_d')
 
         def start_stats():
             ms_v[0] = jnp.full((8, cols), -3.0e38, F32)
@@ -486,21 +531,16 @@
             tgt_v[pl.ds(9, 1), :] = tgt_v[pl.ds(j + 1, 1), :]
         between(j, -1, BLOCKS - 2, start_stats)
 
-        between(j, -1, -1, lambda: loop(nr, lambda i: d_body(i, False, True)))
-        between(j, 0, BLOCKS - 2, lambda: loop(nr, lambda i: d_body(i, True, True)))
-        between(j, BLOCKS - 1, BLOCKS - 1, lambda: loop(nr, lambda i: d_body(i, True, False)))
-        between(j, -1, BLOCKS - 2, lambda: send_stats(j + 1))
-        between(j, -1, BLOCKS - 3, lambda: fetch_block(j + 2))
-        inside(j, lambda b: dz_copy(b).start())
-        inside(j - 1, rs2)
-
-        def finish(b):
-            rs4(b)
-            gather1(dg_v.at[b % 4], dgall_ref, b, g_send, g_recv, g_loc)
-        inside(j - 2, finish)
-        between(j, -1, BLOCKS - 4, lambda: gather2(hpiece(j + 3), hall_ref, j + 3, h_send, h_recv, h_loc))
-        inside(j - 3, lambda b: gather3(dgall_ref, b, g_send, g_recv))
-        between(j, -1, BLOCKS - 3, lambda: project_block(j + 2))
+        between(j, -1, -1, lambda: loop(nr, lambda i: d_body(i, False, True)), 'only_z')
+        between(j, 0, BLOCKS - 2, lambda: loop(nr, lambda i: d_body(i, True, True)), 'full_d')
+        between(j, BLOCKS - 1, BLOCKS - 1, lambda: loop(nr, lambda i: d_body(i, True, False)), 'back')
+        between(j, -1, BLOCKS - 3, lambda: fetch_block(j + 2), 'fetch')
+        between(j, -1, BLOCKS - 2, lambda: send_stats(j + 1), 'stats')
+        inside(j, lambda b: dz_copy(b).start(), 'dzstart')
+        inside(j - 2, last_stage, 'rs4g1')
+        gather_in(2 * j + 1)
+        inside(j - 1, rs2, 'rs2')
+        inside(j - 3, dg3, 'dg3')
         return 0
 
     def gb_copy(r):
@@ -533,7 +573,7 @@
     lax.fori_loop(0, BLOCKS + 4, step_outer, 0)
 
     for b in range(BLOCKS):
-        gather4(dgall_ref, b, g_send, g_recv)
+        gather4(dgall_ref.at[b], g_send.at[b], g_recv.at[b])
     for c in out_copies(BLOCKS - 1):
         c.wait()
     total_ref[...] = jnp.broadcast_to(jnp.sum(tot_v[0:1, :], axis=1, keepdims=True), total_ref.shape)
@@ -565,7 +605,7 @@
     sds = jax.ShapeDtypeStruct
     return pl.pallas_call(
         functools.partial(stream_kernel, dims),
-        out_shape=(sds((BLOCKS, 2, CHIPS, q, depth), BF16), sds((BLOCKS * cols, depth), BF16),
+        out_shape=(sds((BLOCKS, 2, 2, CHIPS, q, depth), BF16), sds((BLOCKS * cols, depth), BF16),
                    sds((rows, BLOCKS * cols), BF16), sds((BLOCKS, 2, CHIPS, q, depth), BF16),
                    sds((BLOCKS, q, depth), F32), sds((BLOCKS, q, depth), BF16),
                    sds((BLOCKS, cols), F32), sds((8, 128), F32), sds((8, depth), F32),
@@ -578,17 +618,17 @@
             pltpu.VMEM((rows, cols), F32), pltpu.VMEM((rows, cols), BF16),
             pltpu.VMEM((2, 2, 2, half, depth), F32), pltpu.VMEM((2, 2, half, depth), F32),
             pltpu.VMEM((2, 2, q, depth), F32), pltpu.VMEM((3, 2, 2, q, depth), F32),
-            pltpu.VMEM((tokens, depth), BF16), pltpu.VMEM((4, q, depth), BF16),
+            pltpu.VMEM((tokens, depth), BF16), pltpu.VMEM((tokens, depth), BF16),
             pltpu.VMEM((4, q, depth), BF16), pltpu.VMEM((q, depth), F32),
             pltpu.VMEM((2, 8, cols), F32), pltpu.VMEM((2, n, 8, cols), F32),
             pltpu.VMEM((n, BLOCKS, cols), jnp.int32), pltpu.VMEM((16, cols), jnp.int32),
             pltpu.VMEM((BLOCKS, cols), F32), pltpu.VMEM((BLOCKS, cols), F32),
             pltpu.VMEM((3, 8, cols), F32), pltpu.VMEM((8, cols), F32), pltpu.VMEM((8, cols), F32),
             pltpu.VMEM((8, depth), F32), pltpu.VMEM((n, 8, depth), F32),
-            dma((3,)), dma((BLOCKS, 8)), dma((BLOCKS, 8)), dma((BLOCKS,)), dma((BLOCKS, 8)), dma((BLOCKS, 8)),
+            dma((3,)), dma((BLOCKS, 2, 8)), dma((BLOCKS, 2, 8)), dma((BLOCKS, 2)), dma((BLOCKS, 8)), dma((BLOCKS, 8)),
             dma((BLOCKS,)), dma((2, n)), dma((2, n)), dma((2,)), dma((2,)), dma((2, 4)), dma((2, 2)),
             dma((2, 2)), dma((3, 2, 2)), pltpu.SemaphoreType.REGULAR,
-            dma((n,)), dma((n,)), dma, dma, dma((8,)), dma((2,)), dma((n,)), dma((n,)),
+            dma((n,)), dma((n,)), dma, dma, dma((4 * CHIPS,)), dma((2,)), dma((n,)), dma((n,)),
             dma((depth // nc,)), dma((2, 2)), dma((depth // nc,)),
         ],
         compiler_params=pltpu.CompilerParams(collective_id=0, has_side_effects=True, vmem_limit_bytes=67043328),
@@ -596,61 +636,148 @@
     )(hidden, w_two, gain, bias, embed, code)
 
 
-def dense_kernel(part_ref, dz_ref, x_ref, h_ref, g_ref, da_ref, go_ref, w_ref, de_ref, dw_ref, dh_ref, x_v, x_sem):
-    i = pl.program_id(0)
+def dense_kernel(part_ref, dzt_ref, xall_ref, aall_ref, gall_ref, da_ref, go_ref, w_ref, de_ref, dw_ref, dh_ref,
+                 w_v, g_v, x_v, h_v, dw_v, dz_v, de_v, st_v, w_sem, g_sem, x_sem, h_sem, dw_sem, dz_sem, de_sem, in_sem, out_sem):
     depth = x_v.shape[1]
-    nc = depth // 4
-    load = pltpu.make_async_copy(x_ref, x_v, x_sem)
-
-    @pl.when(i == 0)
-    def _():
-        load.start()
-
-    @pl.when(i < KEEP)
-    def _():
-        de_ref[...] = part_ref[...]
-
-    @pl.when(i == KEEP)
-    def _():
-        load.wait()
-
-    @pl.when(i >= KEEP)
-    def _():
-        def part(p, _):
-            sl = pl.ds(pl.multiple_of(p * nc, nc), nc)
-            de_ref[:, sl] = jnp.dot(dz_ref[...], x_v[:, sl], preferred_element_type=F32)
-            return 0
-        lax.fori_loop(0, 4, part, 0)
-    dw_ref[...] = lax.dot_general(h_ref[...], g_ref[...], (((0,), (0,)), ((), ())), preferred_element_type=F32)
-    back = lax.dot_general(go_ref[...], w_ref[...], (((1,), (1,)), ((), ())), preferred_element_type=F32)
-    dh_ref[...] = (da_ref[...] + back).astype(BF16)
-
-
-def dense(part, dzt, xall, hall, dgall, da1, dgown, w_two):
+    nc, wb = depth // 4, depth // BLOCKS
+    re = dzt_ref.shape[0] // BLOCKS
+    xr = x_v.shape[0] // BLOCKS
+    todo = BLOCKS - KEEP
+    pieces = BLOCKS + 4 * todo
+    pr = KEEP * re // pieces
+
+    def at(i, size):
+        return pl.ds(pl.multiple_of(i * size, size), size)
+
+    def w_copy(i):
+        return pltpu.make_async_copy(w_ref.at[at(i, nc)], w_v.at[at(i, nc)], w_sem.at[i])
+
+    def h_copy(i):
+        return pltpu.make_async_copy(aall_ref.at[:, 0:h_v.shape[2], at(i, wb)], h_v.at[i % 2], h_sem.at[i % 2])
+
+    def dw_copy(i):
+        return pltpu.make_async_copy(dw_v.at[i % 2], dw_ref.at[at(i, wb)], dw_sem.at[i % 2])
+
+    def x_copy(i):
+        return pltpu.make_async_copy(xall_ref.at[at(i, xr)], x_v.at[at(i, xr)], x_sem.at[i])
+
+    def dz_copy(c):
+        return pltpu.make_async_copy(dzt_ref.at[at(KEEP + c, re)], dz_v.at[c % 2], dz_sem.at[c % 2])
+
+    def de_copy(u):
+        return pltpu.make_async_copy(de_v.at[u % 2], de_ref.at[at(KEEP + u // 4, re), at(u % 4, nc)], de_sem.at[u % 2])
+
+    def pin(t):
+        return pltpu.make_async_copy(part_ref.at[at(t, pr)], st_v.at[t % 4], in_sem.at[t % 4])
+
+    def pout(t):
+        return pltpu.make_async_copy(st_v.at[t % 4], de_ref.at[at(t, pr)], out_sem.at[t % 4])
+
+    def carry(t):
+        pin(t).wait()
+        pout(t).start()
+
+        @pl.when(t >= 2)
+        def _():
+            pout(t - 2).wait()
+
+        @pl.when(t + 2 < pieces)
+        def _():
+            pin(t + 2).start()
+
+    g_load = pltpu.make_async_copy(gall_ref, g_v, g_sem)
+    for i in range(4):
+        w_copy(i).start()
+    g_load.start()
+    h_copy(0).start()
+    h_copy(1).start()
+    pin(0).start()
+    pin(1).start()
+
+    def hidden_part(i, _):
+        w_copy(i).wait()
+        sl = at(i, nc)
+        back = lax.dot_general(go_ref[...], w_v[sl, :], (((1,), (1,)), ((), ())), preferred_element_type=F32)
+        dh_ref[:, sl] = (da_ref[:, sl] + back).astype(BF16)
+        return 0
+    lax.fori_loop(0, 4, hidden_part, 0)
+    g_load.wait()
+
+    def dw_part(i, _):
+        h_copy(i).wait()
+        x_copy(i).start()
+
+        @pl.when(i == BLOCKS - 2)
+        def _():
+            dz_copy(0).start()
+            dz_copy(1).start()
+        carry(i)
+
+        @pl.when(i >= 2)
+        def _():
+            dw_copy(i - 2).wait()
+        h = h_v[i % 2].reshape(g_v.shape[0], wb)
+        dw_v[i % 2] = lax.dot_general(h, g_v[...], (((0,), (0,)), ((), ())), preferred_element_type=F32)
+        dw_copy(i).start()
+
+        @pl.when(i + 2 < BLOCKS)
+        def _():
+            h_copy(i + 2).start()
+        return 0
+    lax.fori_loop(0, BLOCKS, dw_part, 0)
+    for i in range(BLOCKS):
+        x_copy(i).wait()
+
+    def de_part(u, _):
+        c = u // 4
+
+        @pl.when(u % 4 == 0)
+        def _():
+            dz_copy(c).wait()
+        carry(BLOCKS + u)
+
+        @pl.when(u >= 2)
+        def _():
+            de_copy(u - 2).wait()
+        de_v[u % 2] = jnp.dot(dz_v[c % 2], x_v[:, at(u % 4, nc)], preferred_element_type=F32)
+        de_copy(u).start()
+
+        @pl.when(jnp.logical_and(u % 4 == 3, c + 2 < todo))
+        def _():
+            dz_copy(c + 2).start()
+        return 0
+    lax.fori_loop(0, 4 * todo, de_part, 0)
+    for i in (BLOCKS - 2, BLOCKS - 1):
+        dw_copy(i).wait()
+    for i in (4 * todo - 2, 4 * todo - 1):
+        de_copy(i).wait()
+    for t in (pieces - 2, pieces - 1):
+        pout(t).wait()
+
+
+def dense(part, dzt, xall, aall, gall, da1, dgown, w_two):
     rows, kk = dzt.shape
     depth = xall.shape[1]
-    total, tokens = hall.shape[0], da1.shape[0]
-    re, wb = rows // BLOCKS, depth // BLOCKS
+    total, tokens = gall.shape[0], da1.shape[0]
+    re, wb, nc = rows // BLOCKS, depth // BLOCKS, depth // 4
+    pieces = BLOCKS + 4 * (BLOCKS - KEEP)
     sds = jax.ShapeDtypeStruct
-    one = pl.Buffered(buffer_count=1)
+    dma = pltpu.SemaphoreType.DMA
+    any_spec = pl.BlockSpec(memory_space=pl.ANY)
+    vmem = pl.BlockSpec(memory_space=pltpu.VMEM)
     return pl.pallas_call(
         dense_kernel,
-        grid=(BLOCKS,),
         out_shape=(sds((rows, depth), F32), sds((depth, depth), F32), sds((tokens, depth), BF16)),
-        in_specs=[pl.BlockSpec((re, depth), lambda i: (jnp.minimum(i, KEEP - 1), 0)),
-                  pl.BlockSpec((re, kk), lambda i: (jnp.maximum(i, KEEP), 0)),
-                  pl.BlockSpec(memory_space=pl.ANY),
-                  pl.BlockSpec((total, wb), lambda i: (0, i)),
-                  pl.BlockSpec((total, depth), lambda i: (0, 0), pipeline_mode=one),
-                  pl.BlockSpec((tokens, wb), lambda i: (0, i)),
-                  pl.BlockSpec((tokens, depth), lambda i: (0, 0), pipeline_mode=one),
-                  pl.BlockSpec((wb, depth), lambda i: (i, 0))],
-        out_specs=(pl.BlockSpec((re, depth), lambda i: (i, 0)), pl.BlockSpec((wb, depth), lambda i: (i, 0)),
-                   pl.BlockSpec((tokens, wb), lambda i: (0, i))),
-        scratch_shapes=[pltpu.VMEM((kk, depth), BF16), pltpu.SemaphoreType.DMA],
+        in_specs=[any_spec] * 5 + [vmem, vmem, any_spec],
+        out_specs=(any_spec, any_spec, vmem),
+        scratch_shapes=[pltpu.VMEM((depth, depth), BF16), pltpu.VMEM((total, depth), BF16), pltpu.VMEM((kk, depth), BF16),
+                        pltpu.VMEM((2, BLOCKS, total // BLOCKS, wb), BF16), pltpu.VMEM((2, wb, depth), F32),
+                        pltpu.VMEM((2, re, kk), BF16), pltpu.VMEM((2, re, nc), F32),
+                        pltpu.VMEM((4, KEEP * re // pieces, depth), F32),
+                        dma((4,)), dma, dma((BLOCKS,)), dma((2,)), dma((2,)), dma((2,)), dma((2,)), dma((4,)), dma((4,))],
         compiler_params=pltpu.CompilerParams(vmem_limit_bytes=67043328),
         name='dense',
-    )(part, dzt, xall, hall, dgall, da1, dgown, w_two)
+    )(part, dzt, xall, aall, gall, da1, dgown, w_two)
 
 
 def solution(mesh):
@@ -666,9 +793,9 @@
         place = (me % 2) * CHIPS + me // 2
         seat = lax.broadcasted_iota(jnp.int32, (1, 1, 2 * CHIPS, 1), 2) == place
         code = jnp.where(seat, code[:, :, None, :], 0).reshape(BLOCKS, 2 * 2 * CHIPS * q)
-        hall, xall, dzt, dgall, da1, dgown, loss, total, dgb, part = stream(
+        aall, xall, dzt, dgall, da1, dgown, loss, total, dgb, part = stream(
             n, hidden, w_two, ln_scale, ln_shift, embed, code)
-        d_embed, d_w, d_hidden = dense(part, dzt, xall, hall.reshape(n * tokens, depth), dgall.reshape(n * tokens, depth),
+        d_embed, d_w, d_hidden = dense(part, dzt, xall, aall.reshape(BLOCKS, 2 * n * q, depth), dgall.reshape(n * tokens, depth),
                                        da1.reshape(tokens, depth), dgown.reshape(tokens, depth), w_two)
         loss = loss.reshape(BLOCKS, 2, 2 * CHIPS, q)
         mine = lax.dynamic_index_in_dim(loss, place, axis=2, keepdims=False)

time: 396 us -> 376 us (0.949)
  Pallas kernels: 389 us -> 369 us
    pallas_call x1, Pallas kernels: 319 us -> 307 us  [stream(): pl.pallas_call(functools.partial(stream_kernel, dims), out_shape=(sds((BL...]
    pallas_call x1, Pallas kernels: 69.3 us -> 61.9 us  [dense(): pl.pallas_call(dense_kernel, out_shape=(sds((rows, depth), F32), sds((dep...]
where the time goes in v3:
time: 376 us; the launch traced here: 375 us
  Pallas kernels  369 us (98%)
  local copies, waits for them, and re-layouts  4.53 us (1%)
    pallas_call x1, Pallas kernels, stream(): pl.pallas_call(functools.partial(stream_kernel, dims), out_shape=(sds((BL...  307 us
    pallas_call x1, Pallas kernels, dense(): pl.pallas_call(dense_kernel, out_shape=(sds((rows, depth), F32), sds((dep...  61.9 us

profile of v3, /device:TPU:81, one launch (start us, length us, event | category | flops | bytes accessed | tf_op | source)
XLA Modules:
  0.0 375.5 jit_solution(11781044720898645904)
XLA Ops:
  0.7 0.1 broadcast_in_dim.27
  0.7 0.1 broadcast_in_dim.28
  0.8 0.7 multiply_add_fusion
  1.5 0.1 reshape.44
  1.6 0.1 broadcast_in_dim.31
  1.7 0.6 broadcast_select_fusion.code_ref
  2.3 306.9 %stream.1 = (bf16[8,2,2,4,32,2048]{5,4,3,2,1,0:T(8,128)(2,1)}, bf16[4096,2048]{1,0:T(8,128)(2,1)}, bf16[4096,4096]{1,0:T(8,128)(2,1)}, bf16[8,2,4,32,2048]{4,3,2...) custom-call(bf16[256,2048]{1,0:T(8,128)(2,1)} %h_ref.1, ...), custom_call_target="tpu_custom_call" | custom-call | tf_op jit(solution)/shard_map/stream/pallas_call | solution.py:606
  309.2 1.2 slice.9
  310.4 1.5 fusion
  311.9 0.8 reshape.45
  312.8 0.7 reshape.46
  313.4 61.9 %dense.1 = (f32[4096,2048]{1,0:T(8,128)}, f32[2048,2048]{1,0:T(8,128)}, bf16[256,2048]{1,0:T(8,128)(2,1)}) custom-call(f32[2560,2048]{1,0:T(8,128)} %get-tuple-element.22.part_ref, bf16[4096,4096]{1,0:T(8,128)(2,1)} %get-tuple-element.23.dzt_ref, bf16[4096,2048]{1,0:T(8,128)(2,1)} %get-tuple-element.24.xall_ref, bf16[8,512,2048]{2,1,0:T(8,128)(2,1)} %bitcast.13, ...), custom_call_target="tpu_custom_call" | custom-call | tf_op jit(solution)/shard_map/dense/pallas_call | solution.py:768
  (5 shorter events, 0.0 us)
